TPU v7x, 32 devices: a whole 2x2x4 slice. The times are simulated.
32 devices in a mesh: dp: 2 (over x), tp: 4 (over z), cp: 4 (over y, core).
Axes of the slice: x: 2, y: 2, z: 4, core: 2. Of those that a mesh axis runs over, the one named last changes fastest.
Arguments:
- x_chunk: bfloat16 [16, 512, 2048], P('dp', 'cp'), parts along dimension 0
- w_query: bfloat16 [2048, 2048], P(None, 'tp')
- w_key: bfloat16 [2048, 2048], P(None, 'tp')
- w_value: bfloat16 [2048, 2048], P(None, 'tp')
- w_out: bfloat16 [2048, 2048], P('tp')
- q_gain: bfloat16 [2048], P('tp')
- k_gain: bfloat16 [2048], P('tp')
- post_gain: bfloat16 [2048], replicated
- cache_k: bfloat16 [16, 8192, 16, 128], P('dp', 'cp', 'tp'), parts along dimension 0
- cache_v: bfloat16 [16, 8192, 16, 128], P('dp', 'cp', 'tp'), parts along dimension 0
- prefix_len: int32 [16], P('dp'), parts along dimension 0
Outputs:
- output 1: bfloat16 [16, 512, 2048], P('dp', 'cp'), parts along dimension 0
- output 2: bfloat16 [16, 512, 16, 128], P('dp', 'cp', 'tp'), parts along dimension 0
- output 3: bfloat16 [16, 512, 16, 128], P('dp', 'cp', 'tp'), parts along dimension 0
There are 2 independent parts. A program takes and returns all parts, laid end to end along the dimension named above; an argument that names none is the same for every part.
All inputs are finite; a program needn't handle non-finite values.
Results may differ from a plain program's by a relative error of at most 0.00736104.
Values are sent between devices in bfloat16 or wider.
A program may use at most 1 GiB of HBM per device.

v0:
```python
import jax
import jax.numpy as jnp
from jax import lax
from jax.sharding import PartitionSpec as P

NORM_EPS = 1e-6
ROPE_BASE = 500000.0
MASK_VALUE = -1e30


def rope_apply(head_vals, positions):
    head_dim = head_vals.shape[-1]
    half_dim = head_dim // 2
    inv_freq = ROPE_BASE ** (-(jnp.arange(half_dim, dtype=jnp.float32) * 2.0 / head_dim))
    angles = positions.astype(jnp.float32)[..., None] * inv_freq
    cos_tab = jnp.cos(angles)[..., None, :]
    sin_tab = jnp.sin(angles)[..., None, :]
    first_half = head_vals[..., :half_dim]
    second_half = head_vals[..., half_dim:]
    return jnp.concatenate([first_half * cos_tab - second_half * sin_tab, second_half * cos_tab + first_half * sin_tab], axis=-1)


def solution(mesh):
    cp_size = mesh.shape['cp']
    tp_size = mesh.shape['tp']

    def local_step(x_chunk, w_query, w_key, w_value, w_out, q_gain, k_gain, post_gain, cache_k, cache_v, prefix_len):
        batch_rows, chunk_dev, model_dim = x_chunk.shape
        cache_dev = cache_k.shape[1]
        kv_local = cache_k.shape[2]
        head_dim = cache_k.shape[3]
        q_local = w_query.shape[1] // head_dim
        groups = q_local // kv_local
        cp_index = lax.axis_index('cp')
        tokens = x_chunk.reshape(batch_rows * chunk_dev, model_dim)
        q_raw = jnp.dot(tokens, w_query, preferred_element_type=jnp.float32)
        k_raw = jnp.dot(tokens, w_key, preferred_element_type=jnp.float32)
        v_raw = jnp.dot(tokens, w_value, preferred_element_type=jnp.float32)
        square_sums = lax.psum(jnp.stack([jnp.sum(q_raw * q_raw, axis=-1), jnp.sum(k_raw * k_raw, axis=-1)]), 'tp')
        q_inv = lax.rsqrt(square_sums[0] / (w_query.shape[1] * tp_size) + NORM_EPS)
        k_inv = lax.rsqrt(square_sums[1] / (w_key.shape[1] * tp_size) + NORM_EPS)
        q_norm = (q_raw * q_inv[:, None] * q_gain.astype(jnp.float32)).reshape(batch_rows, chunk_dev, q_local, head_dim)
        k_norm = (k_raw * k_inv[:, None] * k_gain.astype(jnp.float32)).reshape(batch_rows, chunk_dev, kv_local, head_dim)
        positions = prefix_len[:, None] + cp_index * chunk_dev + jnp.arange(chunk_dev, dtype=jnp.int32)[None, :]
        q_new = rope_apply(q_norm, positions).astype(jnp.bfloat16).reshape(batch_rows, chunk_dev, kv_local, groups, head_dim)
        chunk_k = rope_apply(k_norm, positions).astype(jnp.bfloat16)
        chunk_v = v_raw.astype(jnp.bfloat16).reshape(batch_rows, chunk_dev, kv_local, head_dim)
        q_all = lax.all_gather(q_new, 'cp', axis=1, tiled=True)
        score_scale = head_dim ** -0.5
        slot_index = cp_index * cache_dev + jnp.arange(cache_dev)
        cache_ok = (slot_index[None, :] < prefix_len[:, None])[:, None, None, None, :]
        key_index = cp_index * chunk_dev + jnp.arange(chunk_dev)

        def block_attention(block_id):
            q_blk = lax.dynamic_slice_in_dim(q_all, block_id * chunk_dev, chunk_dev, axis=1)
            query_index = block_id * chunk_dev + jnp.arange(chunk_dev)
            chunk_ok = (key_index[None, :] <= query_index[:, None])[None, :, None, None, :]
            s_cache = jnp.einsum('bqkgd,btkd->bqkgt', q_blk, cache_k, preferred_element_type=jnp.float32) * score_scale
            s_cache = jnp.where(cache_ok, s_cache, MASK_VALUE)
            s_chunk = jnp.einsum('bqkgd,btkd->bqkgt', q_blk, chunk_k, preferred_element_type=jnp.float32) * score_scale
            s_chunk = jnp.where(chunk_ok, s_chunk, MASK_VALUE)
            row_max = jnp.maximum(jnp.max(s_cache, axis=-1), jnp.max(s_chunk, axis=-1))
            p_cache = jnp.exp(s_cache - row_max[..., None])
            p_chunk = jnp.exp(s_chunk - row_max[..., None])
            den_sum = jnp.sum(p_cache, axis=-1) + jnp.sum(p_chunk, axis=-1)
            num_sum = jnp.einsum('bqkgt,btkd->bqkgd', p_cache.astype(jnp.bfloat16), cache_v, preferred_element_type=jnp.float32)
            num_sum = num_sum + jnp.einsum('bqkgt,btkd->bqkgd', p_chunk.astype(jnp.bfloat16), chunk_v, preferred_element_type=jnp.float32)
            return row_max, den_sum, num_sum

        part_max, part_den, part_num = lax.map(block_attention, jnp.arange(cp_size))
        glob_max = lax.pmax(part_max, 'cp')
        factor = jnp.exp(part_max - glob_max)
        den_total = lax.psum_scatter(part_den * factor, 'cp', scatter_dimension=0, tiled=False)
        num_total = lax.psum_scatter(part_num * factor[..., None], 'cp', scatter_dimension=0, tiled=False)
        attn_out = (num_total / den_total[..., None]).astype(jnp.bfloat16).reshape(batch_rows * chunk_dev, q_local * head_dim)
        mixed_part = jnp.dot(attn_out, w_out, preferred_element_type=jnp.float32)
        mixed_sum = lax.psum(mixed_part, 'tp')
        normed = mixed_sum * lax.rsqrt(jnp.mean(mixed_sum * mixed_sum, axis=-1, keepdims=True) + NORM_EPS) * post_gain.astype(jnp.float32)
        block_out = (x_chunk.astype(jnp.float32) + normed.reshape(batch_rows, chunk_dev, model_dim)).astype(jnp.bfloat16)
        return block_out, chunk_k, chunk_v

    x_spec = P('dp', 'cp', None)
    head_spec = P('dp', 'cp', 'tp', None)
    in_specs = (x_spec, P(None, 'tp'), P(None, 'tp'), P(None, 'tp'), P('tp', None), P('tp'), P('tp'), P(None), head_spec, head_spec, P('dp'))
    out_specs = (x_spec, head_spec, head_spec)
    return jax.shard_map(local_step, mesh=mesh, in_specs=in_specs, out_specs=out_specs, check_vma=False)
```

profile of v0, /device:TPU:0, one launch (start us, length us, event | category | flops | bytes accessed | tf_op | source)
XLA Modules:
  0.0 796.7 jit_solution(3161017833024927764)
XLA Ops:
  8.1 6.7 multiply_reduce_fusion.1
  18.5 13.9 %psum.14 = f32[2,1024]{1,0:T(2,128)S(1)} all-reduce(f32[2,1024]{1,0:T(2,128)S(1)} %pad_maximum_fusion.2), channel_id=1, replica_groups=mesh['dp'=2,'tp'=4,'cp'=4] {'tp'}, use_global_device_ids=true, to_apply=%region_2.0 | all-reduce | flops 2048 | bytes 16384 | tf_op jit(solution)/shard_map/psum | solution.py:39
  59.7 15.2 %copy.50 = bf16[8,2048,4,128]{3,1,2,0:T(8,128)(2,1)} copy(bf16[8,2048,4,128]{3,2,1,0:T(4,128)(2,1)} %param.21) | data formatting | bytes 33554432
  78.4 16.1 %copy.52 = bf16[8,2048,4,128]{3,1,2,0:T(8,128)(2,1)} copy(bf16[8,2048,4,128]{3,2,1,0:T(4,128)(2,1)} %param.22) | data formatting | bytes 33554432
  99.5 248.7 %while.15 = (s32[]{:T(128)}, f32[4,8,128,4,1]{2,1,4,3,0:T(8,128)S(1)}, f32[4,8,128,4,1]{2,4,3,1,0:T(1,128)S(1)}, f32[4,8,128,4,1,128]{5,2,3,1,4,0:T(8,128)}, s32...) while((s32[]{:T(128)}, ...), condition=%wide.region_8.9_spmd.clone, body=%wide.region_3.8_spmd.clone.sunk | while | flops 4659896320 | bytes 166078800 | solution.py:70
  102.5 18.1 %fusion.64 = (f32[8,128,4]{1,2,0:T(4,128)S(1)}, f32[8,4,128,2048]{3,2,1,0:T(8,128)}) fusion(pred[8,2048]{1,0:T(8,128)(4,1)S(1)} %compare_bitcast_fusion.2, bf16[8,2048,4,128]{3,1,2,0:T(8,128)(2,1)} %get-tuple-element.324, bf16[8,128,4,1,128]{4,2,1,0,3:T(4,128)(2,1)S(1)} %constant_dynamic-slice_fusion.2), kind=kOutput, calls=%fused_computation.7.clone.1 | convolution fusion | flops 2172645376 | bytes 51412992 | tf_op jit(solution)/shard_map/while/body/eval_jaxpr/bqkgd,btkd->bqkgt/dot_general | solution.py:58
  121.6 15.2 %fusion.66 = f32[8,128,4]{1,2,0:T(4,128)S(1)} fusion(f32[8,4,128,2048]{3,2,1,0:T(8,128)} %get-tuple-element.282, f32[8,128,4]{1,2,0:T(4,128)S(1)} %max.24, pred[8,2048]{1,0:T(8,128)(4,1)S(1)} %compare_bitcast_fusion.2), kind=kLoop, calls=%fused_computation.6.clone.1 | loop fusion | flops 33550336 | bytes 33603584 | tf_op jit(solution)/shard_map/while/body/eval_jaxpr/reduce_sum | solution.py:65
  137.2 20.4 %fusion.68 = f32[8,4,128,128]{3,2,1,0:T(8,128)} fusion(bf16[8,2048,4,128]{3,1,2,0:T(8,128)(2,1)} %get-tuple-element.326, f32[8,4,128,2048]{3,2,1,0:T(8,128)} %get-tuple-element.282, f32[8,128,4]{1,2,0:T(4,128)S(1)} %max.24, pred[8,2048]{1,0:T(8,128)(4,1)S(1)} %compare_bitcast_fusion.2), kind=kOutput, calls=%fused_computation.9.clone.1 | convolution fusion | flops 2181038080 | bytes 52461568 | tf_op jit(solution)/shard_map/while/body/eval_jaxpr/bqkgt,btkd->bqkgd/dot_general | solution.py:66
  164.6 18.1 %fusion.64 = (f32[8,128,4]{1,2,0:T(4,128)S(1)}, f32[8,4,128,2048]{3,2,1,0:T(8,128)}) fusion(pred[8,2048]{1,0:T(8,128)(4,1)S(1)} %compare_bitcast_fusion.2, bf16[8,2048,4,128]{3,1,2,0:T(8,128)(2,1)} %get-tuple-element.324, bf16[8,128,4,1,128]{4,2,1,0,3:T(4,128)(2,1)S(1)} %constant_dynamic-slice_fusion.2), kind=kOutput, calls=%fused_computation.7.clone.1 | convolution fusion | flops 2172645376 | bytes 51412992 | tf_op jit(solution)/shard_map/while/body/eval_jaxpr/bqkgd,btkd->bqkgt/dot_general | solution.py:58
  183.7 15.2 %fusion.66 = f32[8,128,4]{1,2,0:T(4,128)S(1)} fusion(f32[8,4,128,2048]{3,2,1,0:T(8,128)} %get-tuple-element.282, f32[8,128,4]{1,2,0:T(4,128)S(1)} %max.24, pred[8,2048]{1,0:T(8,128)(4,1)S(1)} %compare_bitcast_fusion.2), kind=kLoop, calls=%fused_computation.6.clone.1 | loop fusion | flops 33550336 | bytes 33603584 | tf_op jit(solution)/shard_map/while/body/eval_jaxpr/reduce_sum | solution.py:65
  199.3 20.4 %fusion.68 = f32[8,4,128,128]{3,2,1,0:T(8,128)} fusion(bf16[8,2048,4,128]{3,1,2,0:T(8,128)(2,1)} %get-tuple-element.326, f32[8,4,128,2048]{3,2,1,0:T(8,128)} %get-tuple-element.282, f32[8,128,4]{1,2,0:T(4,128)S(1)} %max.24, pred[8,2048]{1,0:T(8,128)(4,1)S(1)} %compare_bitcast_fusion.2), kind=kOutput, calls=%fused_computation.9.clone.1 | convolution fusion | flops 2181038080 | bytes 52461568 | tf_op jit(solution)/shard_map/while/body/eval_jaxpr/bqkgt,btkd->bqkgd/dot_general | solution.py:66
  226.8 18.1 %fusion.64 = (f32[8,128,4]{1,2,0:T(4,128)S(1)}, f32[8,4,128,2048]{3,2,1,0:T(8,128)}) fusion(pred[8,2048]{1,0:T(8,128)(4,1)S(1)} %compare_bitcast_fusion.2, bf16[8,2048,4,128]{3,1,2,0:T(8,128)(2,1)} %get-tuple-element.324, bf16[8,128,4,1,128]{4,2,1,0,3:T(4,128)(2,1)S(1)} %constant_dynamic-slice_fusion.2), kind=kOutput, calls=%fused_computation.7.clone.1 | convolution fusion | flops 2172645376 | bytes 51412992 | tf_op jit(solution)/shard_map/while/body/eval_jaxpr/bqkgd,btkd->bqkgt/dot_general | solution.py:58
  245.9 15.2 %fusion.66 = f32[8,128,4]{1,2,0:T(4,128)S(1)} fusion(f32[8,4,128,2048]{3,2,1,0:T(8,128)} %get-tuple-element.282, f32[8,128,4]{1,2,0:T(4,128)S(1)} %max.24, pred[8,2048]{1,0:T(8,128)(4,1)S(1)} %compare_bitcast_fusion.2), kind=kLoop, calls=%fused_computation.6.clone.1 | loop fusion | flops 33550336 | bytes 33603584 | tf_op jit(solution)/shard_map/while/body/eval_jaxpr/reduce_sum | solution.py:65
  261.5 20.4 %fusion.68 = f32[8,4,128,128]{3,2,1,0:T(8,128)} fusion(bf16[8,2048,4,128]{3,1,2,0:T(8,128)(2,1)} %get-tuple-element.326, f32[8,4,128,2048]{3,2,1,0:T(8,128)} %get-tuple-element.282, f32[8,128,4]{1,2,0:T(4,128)S(1)} %max.24, pred[8,2048]{1,0:T(8,128)(4,1)S(1)} %compare_bitcast_fusion.2), kind=kOutput, calls=%fused_computation.9.clone.1 | convolution fusion | flops 2181038080 | bytes 52461568 | tf_op jit(solution)/shard_map/while/body/eval_jaxpr/bqkgt,btkd->bqkgd/dot_general | solution.py:66
  289.0 18.1 %fusion.64 = (f32[8,128,4]{1,2,0:T(4,128)S(1)}, f32[8,4,128,2048]{3,2,1,0:T(8,128)}) fusion(pred[8,2048]{1,0:T(8,128)(4,1)S(1)} %compare_bitcast_fusion.2, bf16[8,2048,4,128]{3,1,2,0:T(8,128)(2,1)} %get-tuple-element.324, bf16[8,128,4,1,128]{4,2,1,0,3:T(4,128)(2,1)S(1)} %constant_dynamic-slice_fusion.2), kind=kOutput, calls=%fused_computation.7.clone.1 | convolution fusion | flops 2172645376 | bytes 51412992 | tf_op jit(solution)/shard_map/while/body/eval_jaxpr/bqkgd,btkd->bqkgt/dot_general | solution.py:58
  308.1 15.2 %fusion.66 = f32[8,128,4]{1,2,0:T(4,128)S(1)} fusion(f32[8,4,128,2048]{3,2,1,0:T(8,128)} %get-tuple-element.282, f32[8,128,4]{1,2,0:T(4,128)S(1)} %max.24, pred[8,2048]{1,0:T(8,128)(4,1)S(1)} %compare_bitcast_fusion.2), kind=kLoop, calls=%fused_computation.6.clone.1 | loop fusion | flops 33550336 | bytes 33603584 | tf_op jit(solution)/shard_map/while/body/eval_jaxpr/reduce_sum | solution.py:65
  323.7 20.4 %fusion.68 = f32[8,4,128,128]{3,2,1,0:T(8,128)} fusion(bf16[8,2048,4,128]{3,1,2,0:T(8,128)(2,1)} %get-tuple-element.326, f32[8,4,128,2048]{3,2,1,0:T(8,128)} %get-tuple-element.282, f32[8,128,4]{1,2,0:T(4,128)S(1)} %max.24, pred[8,2048]{1,0:T(8,128)(4,1)S(1)} %compare_bitcast_fusion.2), kind=kOutput, calls=%fused_computation.9.clone.1 | convolution fusion | flops 2181038080 | bytes 52461568 | tf_op jit(solution)/shard_map/while/body/eval_jaxpr/bqkgt,btkd->bqkgd/dot_general | solution.py:66
  348.9 29.8 %all-reduce.3.cloned.1.call-done = f32[4,8,128,4,1]{2,1,4,3,0:T(8,128)} async-done(((f32[4,8,128,4,1]{2,1,4,3,0:T(8,128)}), f32[4,8,128,4,1]{2,1,4,3,0:T(8,128)}) %all-reduce.3.cloned.1.call-update) | async-done | bytes 65552 | tf_op jit(solution)/shard_map/pmax | solution.py:71
  380.3 7.9 broadcast_multiply_fusion
  388.9 70.2 %reduce-scatter.3.cloned.1.call-done = f32[1,8,128,4,1,128]{5,2,3,1,4,0:T(8,128)} async-done(((f32[4,8,128,4,1,128]{5,2,3,1,4,0:T(8,128)}), f32[1,8,128,4,1,128]{5,2,3,1,4,0:T(8,128)}) %reduce-scatter.3.cloned.1.call-update) | async-done | bytes 2097168 | tf_op jit(solution)/shard_map/reduce_scatter | solution.py:74
  461.9 19.0 %reduce-scatter.5.cloned.1.call-done = f32[1,8,128,4,1]{2,1,4,3,0:T(8,128)} async-done(((f32[4,8,128,4,1]{2,1,4,3,0:T(8,128)}), f32[1,8,128,4,1]{2,1,4,3,0:T(8,128)}) %reduce-scatter.5.cloned.1.call-update) | async-done | bytes 16400 | tf_op jit(solution)/shard_map/reduce_scatter | solution.py:73
  482.5 6.2 fusion.26
  489.4 288.2 %all-reduce.5.cloned.1.call-done = f32[1024,2048]{1,0:T(8,128)} async-done(((f32[1024,2048]{1,0:T(8,128)}), f32[1024,2048]{1,0:T(8,128)}) %all-reduce.5.cloned.1.call-update) | async-done | bytes 8388624 | tf_op jit(solution)/shard_map/psum | solution.py:77
  784.1 6.0 add_convert_fusion
  (140 shorter events, 86.1 us)
Async XLA Ops:
  7.2 474.7 %copy-start = (bf16[512,2048]{1,0:T(8,128)(2,1)S(1)}, bf16[512,2048]{1,0:T(8,128)(2,1)}, u32[]{:S(2)}) copy-start(bf16[512,2048]{1,0:T(8,128)(2,1)} %param.17) | copy-start | bytes 6291460
  7.2 92.3 %all-gather.2.cloned.1.call-start = ((), (), s32[]{:S(2)}) async-start(), calls=%async_computation.2 | async-start | bytes 5242880 | tf_op jit(solution)/shard_map/all_gather | solution.py:48
  8.1 6.7 copy-start.5
  8.1 6.7 copy-start.13
  39.0 2.0 copy-start.10
  39.0 2.1 copy-start.12
  59.4 319.4 %all-reduce.3.cloned.1.call-start = ((), (), s32[]{:S(2)}) async-start(), calls=%async_computation.3 | async-start | bytes 131072 | tf_op jit(solution)/shard_map/pmax | solution.py:71
  59.7 15.2 %copy-start.7 = (bf16[8,128,4,64]{3,2,1,0:T(4,128)(2,1)S(1)}, bf16[8,128,4,64]{3,2,1,0:T(4,128)(2,1)}, u32[]{:S(2)}) copy-start(bf16[8,128,4,64]{3,2,1,0:T(4,128)(2,1)} %get-tuple-element.174) | copy-start | bytes 1572868
  76.2 1.0 copy-start.4
  78.4 16.1 %copy-start.6 = (bf16[8,128,2048]{2,1,0:T(8,128)(2,1)S(1)}, bf16[8,128,2048]{2,1,0:T(8,128)(2,1)}, u32[]{:S(2)}) copy-start(bf16[8,128,2048]{2,1,0:T(8,128)(2,1)} %param.13) | copy-start | bytes 12582916
  78.4 16.1 %copy-start.14 = (bf16[2048,512]{1,0:T(8,128)(2,1)S(1)}, bf16[2048,512]{1,0:T(8,128)(2,1)}, u32[]{:S(2)}) copy-start(bf16[2048,512]{1,0:T(8,128)(2,1)} %param.16) | copy-start | bytes 6291460
  102.5 18.2 %copy-start.8 = (bf16[8,128,4,128]{3,1,2,0:T(8,128)(2,1)S(1)}, bf16[8,128,4,128]{3,1,2,0:T(8,128)(2,1)}, u32[]{:S(2)}) copy-start(bf16[8,128,4,128]{3,1,2,0:T(8,128)(2,1)} %get-tuple-element.325) | copy-start | bytes 3145732 | tf_op jit(solution)/shard_map/while
  121.5 15.2 %copy-start.1 = (f32[8,128,4,1,128]{1,4,2,0,3:T(8,128)}, f32[8,128,4,1,128]{1,4,2,0,3:T(8,128)S(1)}, u32[]{:S(2)}) copy-start(f32[8,128,4,1,128]{1,4,2,0,3:T(8,128)S(1)} %get-tuple-element.283) | copy-start | bytes 6291460 | tf_op jit(solution)/shard_map/while
  164.6 18.2 %copy-start.8 = (bf16[8,128,4,128]{3,1,2,0:T(8,128)(2,1)S(1)}, bf16[8,128,4,128]{3,1,2,0:T(8,128)(2,1)}, u32[]{:S(2)}) copy-start(bf16[8,128,4,128]{3,1,2,0:T(8,128)(2,1)} %get-tuple-element.325) | copy-start | bytes 3145732 | tf_op jit(solution)/shard_map/while
  183.7 15.2 %copy-start.1 = (f32[8,128,4,1,128]{1,4,2,0,3:T(8,128)}, f32[8,128,4,1,128]{1,4,2,0,3:T(8,128)S(1)}, u32[]{:S(2)}) copy-start(f32[8,128,4,1,128]{1,4,2,0,3:T(8,128)S(1)} %get-tuple-element.283) | copy-start | bytes 6291460 | tf_op jit(solution)/shard_map/while
  226.8 18.2 %copy-start.8 = (bf16[8,128,4,128]{3,1,2,0:T(8,128)(2,1)S(1)}, bf16[8,128,4,128]{3,1,2,0:T(8,128)(2,1)}, u32[]{:S(2)}) copy-start(bf16[8,128,4,128]{3,1,2,0:T(8,128)(2,1)} %get-tuple-element.325) | copy-start | bytes 3145732 | tf_op jit(solution)/shard_map/while
  245.8 15.2 %copy-start.1 = (f32[8,128,4,1,128]{1,4,2,0,3:T(8,128)}, f32[8,128,4,1,128]{1,4,2,0,3:T(8,128)S(1)}, u32[]{:S(2)}) copy-start(f32[8,128,4,1,128]{1,4,2,0,3:T(8,128)S(1)} %get-tuple-element.283) | copy-start | bytes 6291460 | tf_op jit(solution)/shard_map/while
  289.0 18.2 %copy-start.8 = (bf16[8,128,4,128]{3,1,2,0:T(8,128)(2,1)S(1)}, bf16[8,128,4,128]{3,1,2,0:T(8,128)(2,1)}, u32[]{:S(2)}) copy-start(bf16[8,128,4,128]{3,1,2,0:T(8,128)(2,1)} %get-tuple-element.325) | copy-start | bytes 3145732 | tf_op jit(solution)/shard_map/while
  308.0 15.2 %copy-start.1 = (f32[8,128,4,1,128]{1,4,2,0,3:T(8,128)}, f32[8,128,4,1,128]{1,4,2,0,3:T(8,128)S(1)}, u32[]{:S(2)}) copy-start(f32[8,128,4,1,128]{1,4,2,0,3:T(8,128)S(1)} %get-tuple-element.283) | copy-start | bytes 6291460 | tf_op jit(solution)/shard_map/while
  348.9 110.2 %reduce-scatter.3.cloned.1.call-start = ((), (), s32[]{:S(2)}) async-start(), calls=%async_computation.4 | async-start | bytes 10485760 | tf_op jit(solution)/shard_map/reduce_scatter | solution.py:74
  388.2 92.6 %reduce-scatter.5.cloned.1.call-start = ((), (), s32[]{:S(2)}) async-start(), calls=%async_computation.5 | async-start | bytes 81920 | tf_op jit(solution)/shard_map/reduce_scatter | solution.py:73
  388.8 388.8 %all-reduce.5.cloned.1.call-start = ((), (), s32[]{:S(2)}) async-start(), calls=%async_computation.6 | async-start | bytes 16777216 | tf_op jit(solution)/shard_map/psum | solution.py:77
  480.9 1.6 copy-start.3
  777.6 5.8 copy-start.2
  (2 other events, 1.3 us)
Sparse Core Ops, SparseCore 0:
  59.5 32.4 all-gather.1
  349.0 29.7 all-reduce.2
  388.4 70.6 reduce-scatter.2
  461.3 19.5 reduce-scatter.4
  488.8 288.7 all-reduce.4
where the time goes:
time: 798 us; the launch traced here: 797 us
  waiting for transfers between devices  408 us (51%)
  matrix products  193 us (24%)
  other arithmetic  99 us (12%)
  local copies, waits for them, and re-layouts  65.7 us (8%)
  between operations  14 us (2%)
  blocking collectives  13.9 us (2%)
    psum x1, waiting for transfers between devices, local_step(): mixed_sum = lax.psum(mixed_part, 'tp')  288 us
    dot_general x4, matrix products, block_attention(): jnp.einsum('bqkgt,btkd->bqkgd', p_cache.astype(jnp.bfloat16), cache_v, pr...  81.7 us
    dot_general x4, matrix products, block_attention(): jnp.einsum('bqkgd,btkd->bqkgt', q_blk, cache_k, preferred_element_type=jn...  72.2 us
    reduce_scatter x1, waiting for transfers between devices, local_step(): lax.psum_scatter(part_num * factor[..., None], 'cp', scatter_dimension=0,...  70.2 us
    reduce_sum x8, other arithmetic, block_attention(): den_sum = jnp.sum(p_cache, axis=-1) + jnp.sum(p_chunk, axis=-1)  62.2 us
    unnamed x36, local copies, waits for them, and re-layouts  49.6 us
    pmax x1, waiting for transfers between devices, local_step(): glob_max = lax.pmax(part_max, 'cp')  29.8 us
    reduce_scatter x1, waiting for transfers between devices, local_step(): lax.psum_scatter(part_den * factor, 'cp', scatter_dimension=0, tiled=False)  19 us
  transfers between devices with their start and end apart: 5, of which 4 were waited for; matrix products, arithmetic and copies ran while one was open for 5% of the time, Pallas kernels for 0%

commit v1 on v0

v1 whole, which is shorter than its diff:
```python
import functools
import jax
import jax.numpy as jnp
from jax import lax
from jax.experimental import pallas as pl
from jax.experimental.pallas import tpu as pltpu
from jax.sharding import PartitionSpec as P

NORM_EPS = 1e-6
ROPE_BASE = 500000.0
MASK_VALUE = -1e30
LOG2E = 1.4426950408889634


def rope_apply(head_vals, positions):
    head_dim = head_vals.shape[-1]
    half_dim = head_dim // 2
    inv_freq = ROPE_BASE ** (-(jnp.arange(half_dim, dtype=jnp.float32) * 2.0 / head_dim))
    angles = positions.astype(jnp.float32)[..., None] * inv_freq
    cos_tab = jnp.cos(angles)[..., None, :]
    sin_tab = jnp.sin(angles)[..., None, :]
    first_half = head_vals[..., :half_dim]
    second_half = head_vals[..., half_dim:]
    return jnp.concatenate([first_half * cos_tab - second_half * sin_tab, second_half * cos_tab + first_half * sin_tab], axis=-1)


def split_heads(raw_ref, wide_ref, out_ref, heads, rows):
    step = wide_ref.shape[0]
    per = step // heads

    def body(i, _):
        wide_ref[...] = raw_ref[pl.ds(i * step, step), :].astype(jnp.float32)
        for h in range(heads):
            out_ref[h, pl.ds(i * per, per), :] = wide_ref[pl.ds(h, per, stride=heads), :].astype(jnp.bfloat16)
        return 0

    lax.fori_loop(0, rows // step, body, 0)


def attend_head(h, q, k_ref, v_ref, kc, vc, s_ref, limit, chunk_ok, tile):
    n_q = q.shape[0]
    n_t = k_ref.shape[1] // tile
    lane = lax.broadcasted_iota(jnp.int32, (1, tile), 1)
    nt = (((1,), (1,)), ((), ()))
    s_c = lax.dot_general(q, kc, nt, preferred_element_type=jnp.float32)
    s_c = jnp.where(chunk_ok, s_c, MASK_VALUE)
    mx = s_c
    for j in range(n_t):
        s = lax.dot_general(q, k_ref[h, j * tile:(j + 1) * tile, :], nt, preferred_element_type=jnp.float32)
        s = jnp.where(lane + j * tile < limit, s, MASK_VALUE)
        s_ref[:, j * tile:(j + 1) * tile] = s
        for u in range(tile // 128):
            mx = jnp.maximum(mx, s[:, u * 128:(u + 1) * 128])
    c = (128 ** -0.5) * LOG2E
    m = jnp.max(mx, axis=1, keepdims=True)
    p = jnp.exp2((s_c - m) * c)
    l = p
    acc = jnp.dot(p.astype(jnp.bfloat16), vc, preferred_element_type=jnp.float32)
    for j in range(n_t):
        p = jnp.exp2((s_ref[:, j * tile:(j + 1) * tile] - m) * c)
        for u in range(tile // 128):
            l = l + p[:, u * 128:(u + 1) * 128]
        acc = acc + jnp.dot(p.astype(jnp.bfloat16), v_ref[h, j * tile:(j + 1) * tile, :], preferred_element_type=jnp.float32)
    l = jnp.sum(l, axis=1, keepdims=True)
    return acc * (1.0 / l), m * c + jnp.log2(l)


def attn_kernel(pre_ref, q_ref, kn_ref, vn_ref, ck_ref, cv_ref, o_ref, lse_ref, wide, k_scr, v_scr, s_scr):
    b = pl.program_id(0)
    cp = lax.axis_index('cp')
    heads = k_scr.shape[0]
    slots = k_scr.shape[1]
    limit = pre_ref[b] - cp * slots
    split_heads(ck_ref.at[0], wide, k_scr, heads, slots * heads)
    split_heads(cv_ref.at[0], wide, v_scr, heads, slots * heads)
    n_q = q_ref.shape[1]
    n_k = kn_ref.shape[1]
    qi = lax.broadcasted_iota(jnp.int32, (n_q, n_k), 0)
    ki = lax.broadcasted_iota(jnp.int32, (n_q, n_k), 1)
    chunk_ok = ki + cp * n_k <= qi
    lane = lax.broadcasted_iota(jnp.int32, (n_q, 128), 1)

    lse_ref[0] = jnp.zeros(lse_ref.shape[1:], jnp.float32)

    def head(h, _):
        col = pl.ds(pl.multiple_of(h * 128, 128), 128)
        o, lse = attend_head(h, q_ref[0, :, col], k_scr, v_scr, kn_ref[0, :, col], vn_ref[0, :, col], s_scr, limit, chunk_ok, 256)
        o_ref[0, :, col] = o.astype(jnp.bfloat16)
        lse_ref[0] = jnp.where(lane == h, lse, lse_ref[0])
        return 0

    lax.fori_loop(0, heads, head, 0)


def attention(prefix_len, q_all, k_new, v_new, cache_k, cache_v):
    rows, n_q, width = q_all.shape
    slots, heads = cache_k.shape[1], cache_k.shape[2]
    ck = cache_k.reshape(rows, slots * heads, 128)
    cv = cache_v.reshape(rows, slots * heads, 128)
    blk = lambda *s: pl.BlockSpec((1,) + s, lambda b, pre: (b, 0, 0))
    spec = pltpu.PrefetchScalarGridSpec(
        num_scalar_prefetch=1, grid=(rows,),
        in_specs=[blk(n_q, width), blk(k_new.shape[1], width), blk(k_new.shape[1], width), blk(slots * heads, 128), blk(slots * heads, 128)],
        out_specs=[blk(n_q, width), blk(n_q, 128)],
        scratch_shapes=[pltpu.VMEM((1024, 128), jnp.float32), pltpu.VMEM((heads, slots, 128), jnp.bfloat16), pltpu.VMEM((heads, slots, 128), jnp.bfloat16), pltpu.VMEM((n_q, slots), jnp.float32)])
    return pl.pallas_call(
        attn_kernel, grid_spec=spec,
        out_shape=[jax.ShapeDtypeStruct((rows, n_q, width), jnp.bfloat16), jax.ShapeDtypeStruct((rows, n_q, 128), jnp.float32)],
        compiler_params=pltpu.CompilerParams(dimension_semantics=("arbitrary",), vmem_limit_bytes=56 << 20),
        cost_estimate=pl.CostEstimate(flops=4 * rows * n_q * slots * width, bytes_accessed=4 * rows * slots * width, transcendentals=rows * n_q * slots * heads),
        name="attn")(prefix_len, q_all, k_new, v_new, ck, cv)


def solution(mesh):
    cp_size = mesh.shape['cp']
    tp_size = mesh.shape['tp']

    def local_step(x_chunk, w_query, w_key, w_value, w_out, q_gain, k_gain, post_gain, cache_k, cache_v, prefix_len):
        batch_rows, chunk_dev, model_dim = x_chunk.shape
        heads = cache_k.shape[2]
        head_dim = cache_k.shape[3]
        width = heads * head_dim
        cp_index = lax.axis_index('cp')
        tokens = x_chunk.reshape(batch_rows * chunk_dev, model_dim)
        q_raw = jnp.dot(tokens, w_query, preferred_element_type=jnp.float32)
        k_raw = jnp.dot(tokens, w_key, preferred_element_type=jnp.float32)
        v_raw = jnp.dot(tokens, w_value, preferred_element_type=jnp.float32)
        square_sums = lax.psum(jnp.stack([jnp.sum(q_raw * q_raw, axis=-1), jnp.sum(k_raw * k_raw, axis=-1)]), 'tp')
        q_inv = lax.rsqrt(square_sums[0] / (width * tp_size) + NORM_EPS)
        k_inv = lax.rsqrt(square_sums[1] / (width * tp_size) + NORM_EPS)
        q_norm = (q_raw * q_inv[:, None] * q_gain.astype(jnp.float32)).reshape(batch_rows, chunk_dev, heads, head_dim)
        k_norm = (k_raw * k_inv[:, None] * k_gain.astype(jnp.float32)).reshape(batch_rows, chunk_dev, heads, head_dim)
        positions = prefix_len[:, None] + cp_index * chunk_dev + jnp.arange(chunk_dev, dtype=jnp.int32)[None, :]
        q_new = rope_apply(q_norm, positions).astype(jnp.bfloat16).reshape(batch_rows, chunk_dev, width)
        k_new = rope_apply(k_norm, positions).astype(jnp.bfloat16).reshape(batch_rows, chunk_dev, width)
        v_new = v_raw.astype(jnp.bfloat16).reshape(batch_rows, chunk_dev, width)
        q_all = lax.all_gather(q_new, 'cp', axis=1, tiled=True)
        o_part, lse = attention(prefix_len, q_all, k_new, v_new, cache_k, cache_v)
        o_part = lax.all_to_all(o_part.reshape(batch_rows, cp_size, chunk_dev, width), 'cp', 1, 1)
        lse = lax.all_to_all(lse[:, :, :heads].reshape(batch_rows, cp_size, chunk_dev, heads), 'cp', 1, 1)
        lse = lse - jnp.max(lse, axis=1, keepdims=True)
        wt = jnp.exp2(lse)
        wt = wt / jnp.sum(wt, axis=1, keepdims=True)
        o = jnp.sum(o_part.astype(jnp.float32).reshape(batch_rows, cp_size, chunk_dev, heads, head_dim) * wt[..., None], axis=1)
        attn_out = o.astype(jnp.bfloat16).reshape(batch_rows * chunk_dev, width)
        mixed = jnp.dot(attn_out, w_out, preferred_element_type=jnp.float32).astype(jnp.bfloat16)
        mixed = lax.all_to_all(mixed.reshape(tp_size, -1, model_dim), 'tp', 0, 0)
        mixed = jnp.sum(mixed.astype(jnp.float32), axis=0)
        normed = mixed * lax.rsqrt(jnp.mean(mixed * mixed, axis=-1, keepdims=True) + NORM_EPS) * post_gain.astype(jnp.float32)
        tp_index = lax.axis_index('tp')
        n = tokens.shape[0] // tp_size
        mine = lax.dynamic_slice_in_dim(tokens, tp_index * n, n, axis=0)
        out = (mine.astype(jnp.float32) + normed).astype(jnp.bfloat16)
        block_out = lax.all_gather(out, 'tp', axis=0, tiled=True).reshape(x_chunk.shape)
        return block_out, k_new.reshape(batch_rows, chunk_dev, heads, head_dim), v_new.reshape(batch_rows, chunk_dev, heads, head_dim)

    x_spec = P('dp', 'cp', None)
    head_spec = P('dp', 'cp', 'tp', None)
    in_specs = (x_spec, P(None, 'tp'), P(None, 'tp'), P(None, 'tp'), P('tp', None), P('tp'), P('tp'), P(None), head_spec, head_spec, P('dp'))
    out_specs = (x_spec, head_spec, head_spec)
    return jax.shard_map(local_step, mesh=mesh, in_specs=in_specs, out_specs=out_specs, check_vma=False)
```

time: 798 us -> 462 us (0.58)
  waiting for transfers between devices: 408 us -> 208 us
  matrix products: 193 us -> 21.1 us
  Pallas kernels: 0 us -> 110 us
  other arithmetic: 99 us -> 27.4 us
  starting transfers between devices: 0.42 us -> 13.4 us
  local copies, waits for them, and re-layouts: 65.7 us -> 53.2 us
    psum x1 -> x0, waiting for transfers between devices: 288 us -> none  [local_step(): mixed_sum = lax.psum(mixed_part, 'tp')]
    dot_general x17 -> x1, matrix products: 180 us -> 4.36 us  [local_step(): jnp.dot(attn_out, w_out, preferred_element_type=jnp.float32)]
    all_to_all x0 -> x3, waiting for transfers between devices: none -> 119 us  [the longest x1 92.8 us: local_step(): mixed = lax.all_to_all(mixed.reshape(tp_size, -1, model_dim), 'tp', 0, 0)]
    pallas_call x0 -> x1, Pallas kernels: none -> 110 us  [attention(): pl.pallas_call(attn_kernel, grid_spec=spec, out_shape=[jax.ShapeDtypeStru...]
    reduce_scatter x2 -> x0, waiting for transfers between devices: 89.1 us -> none  [the longest x1 70.2 us: local_step(): lax.psum_scatter(part_num * factor[..., None], 'cp', scatter_dimension=0,...]
    all_gather x0 -> x1, waiting for transfers between devices: none -> 77.7 us  [local_step(): lax.all_gather(out, 'tp', axis=0, tiled=True).reshape(x_chunk.shape)]
    reduce_sum x9 -> x4, other arithmetic: 66.4 us -> 9.53 us  [the longest x1 6.04 us: local_step(): jnp.sum(o_part.astype(jnp.float32).reshape(batch_rows, cp_size, chunk_dev...]
    unnamed x36 -> x25, local copies, waits for them, and re-layouts: 49.6 us -> 17.2 us
  transfers between devices with their start and end apart: 5 -> 5, of which waited for: 4 -> 4; matrix products, arithmetic and copies ran while one was open for 5% -> 11% of each run, Pallas kernels for 0% -> 0%
where the time goes in v1:
time: 462 us; the launch traced here: 461 us
  waiting for transfers between devices  208 us (45%)
  Pallas kernels  110 us (24%)
  local copies, waits for them, and re-layouts  53.2 us (12%)
  other arithmetic  27.4 us (6%)
  matrix products  21.1 us (5%)
  between operations  14.3 us (3%)
  blocking collectives  13.7 us (3%)
  starting transfers between devices  13.4 us (3%)
    pallas_call x1, Pallas kernels, attention(): pl.pallas_call(attn_kernel, grid_spec=spec, out_shape=[jax.ShapeDtypeStru...  110 us
    all_to_all x1, waiting for transfers between devices, local_step(): mixed = lax.all_to_all(mixed.reshape(tp_size, -1, model_dim), 'tp', 0, 0)  92.8 us
    all_gather x1, waiting for transfers between devices, local_step(): lax.all_gather(out, 'tp', axis=0, tiled=True).reshape(x_chunk.shape)  77.7 us
    all_to_all x1, waiting for transfers between devices, local_step(): lax.all_to_all(o_part.reshape(batch_rows, cp_size, chunk_dev, width), 'cp...  26.6 us
    mul x2, local copies, waits for them, and re-layouts, local_step(): o_part.astype(jnp.float32)  19.2 us
    unnamed x25, local copies, waits for them, and re-layouts  17.2 us
    psum x1, blocking collectives, local_step(): lax.psum(jnp.stack([jnp.sum(q_raw * q_raw, axis=-1), jnp.sum(k_raw * k_ra...  13.7 us
    all_gather x1, waiting for transfers between devices, local_step(): q_all = lax.all_gather(q_new, 'cp', axis=1, tiled=True)  10.8 us
  transfers between devices with their start and end apart: 5, of which 4 were waited for; matrix products, arithmetic and copies ran while one was open for 11% of the time, Pallas kernels for 0%

profile of v1, /device:TPU:0, one launch (start us, length us, event | category | flops | bytes accessed | tf_op | source)
XLA Modules:
  0.0 460.7 jit_solution(6443609609595143226)
XLA Ops:
  7.3 6.7 %multiply_reduce_fusion.3 = (f32[1024]{0:T(1024)S(1)}, f32[1024,512]{0,1:T(8,128)}) fusion(bf16[1024,2048]{1,0:T(8,128)(2,1)} %bitcast.44, bf16[2048,512]{1,0:T(8,128)(2,1)} %param.12), kind=kOutput, calls=%fused_computation.13 | convolution fusion | flops 2148531200 | bytes 8392704 | tf_op jit(solution)/shard_map/dot_general | solution.py:125
  14.0 3.8 multiply_reduce_fusion.2
  17.8 13.7 %psum.7 = f32[2,1024]{1,0:T(2,128)S(1)} all-reduce(f32[2,1024]{1,0:T(2,128)S(1)} %pad_maximum_fusion.1), channel_id=1, replica_groups=mesh['dp'=2,'tp'=4,'cp'=4] {'tp'}, use_global_device_ids=true, to_apply=%region_2.0 | all-reduce | flops 2048 | bytes 16384 | tf_op jit(solution)/shard_map/psum | solution.py:128
  35.1 3.2 copy.25
  42.1 2.9 subtract_convert_fusion
  53.5 3.1 copy.27
  56.7 3.2 copy.28
  65.4 6.2 %convolution_convert_fusion.1 = bf16[1024,512]{1,0:T(8,128)(2,1)} fusion(bf16[1024,2048]{1,0:T(8,128)(2,1)} %bitcast.45, bf16[2048,512]{1,0:T(8,128)(2,1)} %param.14), kind=kOutput, calls=%fused_computation.14 | convolution fusion | flops 2148007936 | bytes 7340032 | tf_op jit(solution)/shard_map/dot_general | solution.py:127
  71.6 10.8 %all-gather.3.cloned.1.call-done.q_ref = bf16[8,512,512]{2,1,0:T(8,128)(2,1)} async-done(((bf16[8,128,512]{2,1,0:T(8,128)(2,1)}), bf16[8,512,512]{2,1,0:T(8,128)(2,1)}) %all-gather.3.cloned.1.call-update) | async-done | bytes 4194320 | tf_op jit(solution)/shard_map/all_gather | solution.py:137
  82.4 109.7 %attn.1 = (bf16[8,512,512]{2,1,0:T(8,128)(2,1)}, f32[8,512,128]{2,1,0:T(8,128)}) custom-call(s32[8]{0:T(128)} %pre_ref.1, bf16[8,512,512]{2,1,0:T(8,128)(2,1)} %all-gather.3.cloned.1.call-done.q_ref, bf16[8,128,512]{2,1,0:T(8,128)(2,1)} %convert_element_type.60.kn_ref, bf16[8,128,512]{2,1,0:T(8,128)(2,1)} %bitcast.42, bf16[8,8192,128]{2,1,0:T(8,128)(2,1)} %bitcast.52, ...), custom_call_target="tpu_custom_call" | custom-call | flops 17179869184 | bytes 33554432 | tf_op jit(solution)/shard_map/attn/pallas_call | solution.py:106
  192.1 2.8 copy.23
  194.9 3.3 all-to-all-start.1
  198.2 4.6 copy.22
  202.8 5.1 %all-to-all-start = ((bf16[8,4,128,512]{3,2,0,1:T(8,128)(2,1)}), bf16[8,4,128,512]{3,2,0,1:T(8,128)(2,1)}, u32[]{:S(2)}, u32[]{:S(2)}) async-start(bf16[8,4,128,512]{3,2,0,1:T(8,128)(2,1)} %copy.22), calls=%async_computation | async-start | bytes 8388608 | tf_op jit(solution)/shard_map/all_to_all | solution.py:139
  210.0 8.9 %mul.181 = f32[8,4,128,4,128]{4,3,2,0,1:T(4,128)} broadcast(f32[8,4,128,4]{3,2,0,1:T(8,128)} %copy.24), dimensions={0,1,2,3} | broadcast | bytes 8454144 | tf_op jit(solution)/shard_map/mul | solution.py:144
  218.8 10.3 %mul.182 = f32[8,4,128,512]{3,2,0,1:T(8,128)} reshape(f32[8,4,128,4,128]{4,3,2,0,1:T(4,128)} %mul.181) | data formatting | bytes 16777216 | tf_op jit(solution)/shard_map/mul | solution.py:144
  229.1 26.6 %all-to-all-done = bf16[8,4,128,512]{3,2,0,1:T(8,128)(2,1)} async-done(((bf16[8,4,128,512]{3,2,0,1:T(8,128)(2,1)}), bf16[8,4,128,512]{3,2,0,1:T(8,128)(2,1)}, u32[]{:S(2)}, u32[]{:S(2)}) %all-to-all-start) | async-done | bytes 4194336 | tf_op jit(solution)/shard_map/all_to_all | solution.py:139
  255.8 6.0 %multiply_reduce_fusion = bf16[8,128,512]{2,1,0:T(8,128)(2,1)S(1)} fusion(f32[8,4,128,512]{3,2,0,1:T(8,128)} %mul.182, bf16[8,4,128,512]{3,2,0,1:T(8,128)(2,1)} %all-to-all-done), kind=kLoop, calls=%fused_computation.1 | loop fusion | flops 5767168 | bytes 13631488 | tf_op jit(solution)/shard_map/reduce_sum | solution.py:144
  261.8 4.4 convolution_convert_fusion
  266.2 5.0 %all-to-all-start.2 = ((bf16[4,256,2048]{2,1,0:T(8,128)(2,1)}), bf16[4,256,2048]{2,1,0:T(8,128)(2,1)}, u32[]{:S(2)}, u32[]{:S(2)}) async-start(bf16[4,256,2048]{2,1,0:T(8,128)(2,1)} %bitcast.38), calls=%async_computation.2 | async-start | bytes 8388608 | tf_op jit(solution)/shard_map/all_to_all | solution.py:147
  271.2 92.8 %all-to-all-done.2 = bf16[4,256,2048]{2,1,0:T(8,128)(2,1)} async-done(((bf16[4,256,2048]{2,1,0:T(8,128)(2,1)}), bf16[4,256,2048]{2,1,0:T(8,128)(2,1)}, u32[]{:S(2)}, u32[]{:S(2)}) %all-to-all-start.2) | async-done | bytes 4194336 | tf_op jit(solution)/shard_map/all_to_all | solution.py:147
  364.0 3.3 convert_reduce_fusion
  371.4 77.7 %all-gather.5.cloned.1.call-done = bf16[1024,2048]{1,0:T(8,128)(2,1)} async-done(((bf16[256,2048]{1,0:T(8,128)(2,1)}), bf16[1024,2048]{1,0:T(8,128)(2,1)}) %all-gather.5.cloned.1.call-update) | async-done | bytes 4194320 | tf_op jit(solution)/shard_map/all_gather | solution.py:154
  449.1 4.8 %copy.32 = bf16[8,128,2048]{2,1,0:T(8,128)(2,1)} copy(bf16[8,128,2048]{2,1,0:T(8,128)(2,1)} %bitcast.40) | data formatting | bytes 8388608
  (52 shorter events, 27.6 us)
Async XLA Ops:
  7.2 254.6 %copy-start = (bf16[512,2048]{1,0:T(8,128)(2,1)S(1)}, bf16[512,2048]{1,0:T(8,128)(2,1)}, u32[]{:S(2)}) copy-start(bf16[512,2048]{1,0:T(8,128)(2,1)} %param.15) | copy-start | bytes 6291460
  7.2 75.2 %all-gather.3.cloned.1.call-start = ((), (), s32[]{:S(2)}) async-start(), calls=%async_computation.3 | async-start | bytes 5242880 | tf_op jit(solution)/shard_map/all_gather | solution.py:137
  7.2 6.7 %copy-start.3 = (bf16[8,128,2048]{2,1,0:T(8,128)(2,1)S(1)}, bf16[8,128,2048]{2,1,0:T(8,128)(2,1)}, u32[]{:S(2)}) copy-start(bf16[8,128,2048]{2,1,0:T(8,128)(2,1)} %param.11) | copy-start | bytes 12582916
  7.3 6.7 %copy-start.7 = (bf16[2048,512]{1,0:T(8,128)(2,1)S(1)}, bf16[2048,512]{1,0:T(8,128)(2,1)}, u32[]{:S(2)}) copy-start(bf16[2048,512]{1,0:T(8,128)(2,1)} %param.13) | copy-start | bytes 6291460
  14.0 17.5 %copy-start.8 = (s32[8]{0:T(128)S(1)}, s32[8]{0:T(128)}, u32[]{:S(2)}) copy-start(s32[8]{0:T(128)} %pre_ref.1) | copy-start | bytes 100
  14.0 17.6 %copy-start.5 = (bf16[512]{0:T(512)(128)(2,1)S(1)}, bf16[512]{0:T(512)(128)(2,1)}, u32[]{:S(2)}) copy-start(bf16[512]{0:T(512)(128)(2,1)} %param.16) | copy-start | bytes 3076
  47.4 2.3 copy-start.6
  64.0 7.6 %copy-start.1 = (bf16[8,128,4,128]{3,2,1,0:T(4,128)(2,1)}, bf16[8,128,4,128]{3,2,1,0:T(4,128)(2,1)S(1)}, u32[]{:S(2)}) copy-start(bf16[8,128,4,128]{3,2,1,0:T(4,128)(2,1)S(1)} %maximum_convert_fusion) | copy-start | bytes 3145732
  194.9 7.9 %all-to-all-start.1 = ((f32[8,4,128,4]{2,0,3,1:T(8,128)}), f32[8,4,128,4]{2,0,3,1:T(8,128)S(1)}, u32[]{:S(2)}, u32[]{:S(2)}) async-start(f32[8,4,128,4]{2,0,3,1:T(8,128)} %copy.23), calls=%async_computation.1 | async-start | bytes 131072 | tf_op jit(solution)/shard_map/all_to_all | solution.py:140
  202.8 53.0 %all-to-all-start = ((bf16[8,4,128,512]{3,2,0,1:T(8,128)(2,1)}), bf16[8,4,128,512]{3,2,0,1:T(8,128)(2,1)}, u32[]{:S(2)}, u32[]{:S(2)}) async-start(bf16[8,4,128,512]{3,2,0,1:T(8,128)(2,1)} %copy.22), calls=%async_computation | async-start | bytes 8388608 | tf_op jit(solution)/shard_map/all_to_all | solution.py:139
  266.2 5.0 %copy-start.4 = (bf16[2048]{0:T(1024)(128)(2,1)S(1)}, bf16[2048]{0:T(1024)(128)(2,1)}, u32[]{:S(2)}) copy-start(bf16[2048]{0:T(1024)(128)(2,1)} %param.18) | copy-start | bytes 12292
  266.2 97.9 %all-to-all-start.2 = ((bf16[4,256,2048]{2,1,0:T(8,128)(2,1)}), bf16[4,256,2048]{2,1,0:T(8,128)(2,1)}, u32[]{:S(2)}, u32[]{:S(2)}) async-start(bf16[4,256,2048]{2,1,0:T(8,128)(2,1)} %bitcast.38), calls=%async_computation.2 | async-start | bytes 8388608 | tf_op jit(solution)/shard_map/all_to_all | solution.py:147
  271.2 177.9 %all-gather.5.cloned.1.call-start = ((), (), s32[]{:S(2)}) async-start(), calls=%async_computation.4 | async-start | bytes 5242880 | tf_op jit(solution)/shard_map/all_gather | solution.py:154
  367.5 2.7 copy-start.2
Sparse Core Ops, SparseCore 0:
  49.9 32.4 all-gather.2
  370.4 78.6 all-gather.4

commit v2 on v0

v2 whole, which is shorter than its diff:
```python
import functools
import jax
import jax.numpy as jnp
from jax import lax
from jax.experimental import pallas as pl
from jax.experimental.pallas import tpu as pltpu
from jax.sharding import PartitionSpec as P

NORM_EPS = 1e-6
ROPE_BASE = 500000.0
MASK_VALUE = -1e30
LOG2E = 1.4426950408889634
MESH = pl.DeviceIdType.MESH
NT = (((1,), (1,)), ((), ()))
F32 = jnp.float32
BF16 = jnp.bfloat16


def split_heads(raw_ref, wide_ref, out_ref, heads, rows):
    step = wide_ref.shape[0]
    per = step // heads

    def body(i, _):
        wide_ref[...] = raw_ref[pl.ds(i * step, step), :].astype(F32)
        for h in range(heads):
            out_ref[h, pl.ds(i * per, per), :] = wide_ref[pl.ds(h, per, stride=heads), :].astype(BF16)
        return 0

    lax.fori_loop(0, rows // step, body, 0)


def attend_head(h, q, k_ref, v_ref, kc, vc, s_ref, limit, bias, tile):
    n_t = k_ref.shape[1] // tile
    lane = lax.broadcasted_iota(jnp.int32, (1, tile), 1)
    s_c = lax.dot_general(q, kc, NT, preferred_element_type=F32)
    s_c = jnp.where(bias >= 0, s_c, MASK_VALUE)
    mx = s_c
    for j in range(n_t):
        s = lax.dot_general(q, k_ref[h, j * tile:(j + 1) * tile, :], NT, preferred_element_type=F32)
        s = jnp.where(lane + j * tile < limit, s, MASK_VALUE)
        s_ref[:, j * tile:(j + 1) * tile] = s
        for u in range(tile // 128):
            mx = jnp.maximum(mx, s[:, u * 128:(u + 1) * 128])
    c = (128 ** -0.5) * LOG2E
    m = jnp.max(mx, axis=1, keepdims=True)
    p = jnp.exp2((s_c - m) * c)
    l = p
    acc = jnp.dot(p.astype(BF16), vc, preferred_element_type=F32)
    for j in range(n_t):
        p = jnp.exp2((s_ref[:, j * tile:(j + 1) * tile] - m) * c)
        for u in range(tile // 128):
            l = l + p[:, u * 128:(u + 1) * 128]
        acc = acc + jnp.dot(p.astype(BF16), v_ref[h, j * tile:(j + 1) * tile, :], preferred_element_type=F32)
    l = jnp.sum(l, axis=1, keepdims=True)
    return acc * (1.0 / l), m * c + jnp.log2(l)


def step_kernel(n_tp, pre_ref, x_hbm, wq_hbm, wk_hbm, wv_hbm, wo_hbm, qg_ref, kg_ref, pg_ref, cos_ref, sin_ref, ck_hbm, cv_hbm,
                out_hbm, ok_hbm, ov_hbm,
                x_v, wqkv, wf, q_buf, kn, vn, rA, rB, rC, lA, lB, lC, c_o, c_l, l_buf, o_all, st,
                raw, wide, k_scr, v_scr, s_scr, bias, lse_scr,
                in_sem, kv_sem, out_sem, st_s, st_r, q_s, q_r, p_s, p_r, z_s, z_r, w_s, w_r):
    rows, toks, model = x_v.shape
    heads, slots = k_scr.shape[0], k_scr.shape[1]
    width = heads * 128
    groups = rows // 2
    gt = 2 * toks
    dp, z, me = lax.axis_index('dp'), lax.axis_index('tp'), lax.axis_index('cp')
    partner = me + 1 - 2 * (me % 2)
    counter = (me + 2) % 4
    diag = 3 - me
    last = n_tp - 1
    piece = wo_hbm.shape[0] // 8

    def remote(src, dst, ss, rs, **dev):
        return pltpu.make_async_remote_copy(src_ref=src, dst_ref=dst, send_sem=ss, recv_sem=rs, device_id=dev, device_id_type=MESH)

    loads = [pltpu.make_async_copy(x_hbm, x_v, in_sem.at[0])]
    for i, w in enumerate((wq_hbm, wk_hbm, wv_hbm)):
        loads.append(pltpu.make_async_copy(w, wqkv.at[i], in_sem.at[1 + i]))
    js = pl.ds(pl.multiple_of((dp * 4 + me) * piece, piece), piece)
    w_local = pltpu.make_async_copy(wo_hbm.at[js, :], wf.at[z, js, :], in_sem.at[4])
    w_local.start()
    for cpy in loads:
        cpy.start()

    def kv_copies(b):
        par = b % 2
        return (pltpu.make_async_copy(ck_hbm.at[b], raw.at[par, 0], kv_sem.at[par, 0]),
                pltpu.make_async_copy(cv_hbm.at[b], raw.at[par, 1], kv_sem.at[par, 1]))

    for cpy in kv_copies(0):
        cpy.start()

    barrier = pltpu.get_barrier_semaphore()
    for i in range(1, n_tp):
        pl.semaphore_signal(barrier, inc=1, device_id={'tp': (z + i) % n_tp}, device_id_type=MESH)
    pl.semaphore_signal(barrier, inc=1, device_id={'cp': partner}, device_id_type=MESH)
    pl.semaphore_signal(barrier, inc=1, device_id={'cp': counter}, device_id_type=MESH)
    pl.semaphore_signal(barrier, inc=1, device_id={'dp': 1 - dp}, device_id_type=MESH)
    pl.semaphore_wait(barrier, n_tp + 2)

    def hop(buf, send, recv, k, wait_only=False, start=True):
        if k > 1:
            @pl.when(z - (k - 1) >= 0)
            def _():
                remote(buf(z - (k - 1)), buf(z - (k - 1)), send(0, k - 2), recv(0, k - 2), tp=z).wait_recv()

            @pl.when(z + (k - 1) <= last)
            def _():
                remote(buf(z + (k - 1)), buf(z + (k - 1)), send(1, k - 2), recv(1, k - 2), tp=z).wait_recv()
        if k <= last:
            @pl.when((z - (k - 1) >= 0) & (z < last))
            def _():
                remote(buf(z - (k - 1)), buf(z - (k - 1)), send(0, k - 1), recv(0, k - 1), tp=z + 1).start()

            @pl.when((z + (k - 1) <= last) & (z > 0))
            def _():
                remote(buf(z + (k - 1)), buf(z + (k - 1)), send(1, k - 1), recv(1, k - 1), tp=z - 1).start()

    def hop_sent(buf, send, recv):
        for k in range(1, last + 1):
            @pl.when((z - (k - 1) >= 0) & (z < last))
            def _():
                remote(buf(z - (k - 1)), buf(z - (k - 1)), send(0, k - 1), recv(0, k - 1), tp=z).wait_send()

            @pl.when((z + (k - 1) <= last) & (z > 0))
            def _():
                remote(buf(z + (k - 1)), buf(z + (k - 1)), send(1, k - 1), recv(1, k - 1), tp=z).wait_send()

    def w_hop(k):
        hop(lambda o: wf.at[o, js, :], lambda d, i: w_s.at[d * last + i], lambda d, i: w_r.at[d * last + i], k)

    def o_hop(b, k):
        hop(lambda o: o_all.at[o, b], lambda d, i: z_s.at[b, d * last + i], lambda d, i: z_r.at[b, d * last + i], k)

    w_local.wait()
    w_hop(1)

    qi = lax.broadcasted_iota(jnp.int32, (toks, toks), 0)
    ki = lax.broadcasted_iota(jnp.int32, (toks, toks), 1)
    for s, blk in enumerate((me, partner, counter, diag)):
        bias[s * toks:(s + 1) * toks, :] = jnp.where(ki - qi <= (blk - me) * toks, 0.0, -1.0)
    lse_scr[...] = jnp.zeros(lse_scr.shape, F32)

    for cpy in loads:
        cpy.wait()

    def st_copy(g, i):
        return remote(st.at[g, 0], st.at[g, i], st_s.at[g, i - 1], st_r.at[g, i - 1], tp=(z + i) % n_tp)

    def q_copy(b, i):
        src = q_buf.at[b, pl.ds(0 if i < 2 else 2 * toks, toks), :]
        dst = q_buf.at[b, pl.ds((i + 1) * toks, toks), :]
        return remote(src, dst, q_s.at[b, i], q_r.at[b, i], cp=counter if i == 1 else partner)

    def project(g):
        xg = x_v[pl.ds(2 * g, 2)].reshape(gt, model)
        cols = pl.ds(pl.multiple_of(g * width, width), width)
        q = jnp.dot(xg, wqkv[0], preferred_element_type=F32)
        s_scr[0:gt, cols] = q
        k = jnp.dot(xg, wqkv[1], preferred_element_type=F32)
        s_scr[gt:2 * gt, cols] = k
        lane = lax.broadcasted_iota(jnp.int32, (gt, 128), 1)
        sq = jnp.sum(q * q, axis=1, keepdims=True)
        sk = jnp.sum(k * k, axis=1, keepdims=True)
        sums = jnp.where(lane == 0, sq, jnp.where(lane == 1, sk, 0.0))
        st[g, 0] = jnp.transpose(sums)[0:8, :]
        v = jnp.dot(xg, wqkv[2], preferred_element_type=F32)
        for i in range(1, n_tp):
            st_copy(g, i).start()
        vn[pl.ds(2 * g, 2)] = v.astype(BF16).reshape(2, toks, width)

    def normalize(g):
        for i in range(1, n_tp):
            st_copy(g, i).wait_recv()
        tot = st[g, 0]
        for i in range(1, n_tp):
            tot = tot + st[g, i]
        inv = jnp.transpose(lax.rsqrt(tot / (width * n_tp) + NORM_EPS))
        for t, (gain, base) in enumerate(((qg_ref, 0), (kg_ref, gt))):
            for h in range(heads):
                u = s_scr[base:base + gt, pl.ds(pl.multiple_of(g * width + h * 128, 128), 128)]
                u = u * inv[:, t:t + 1] * gain[0:1, h * 128:(h + 1) * 128].astype(F32)
                cos = cos_ref[pl.ds(2 * g, 2)].reshape(gt, 128)
                sin = sin_ref[pl.ds(2 * g, 2)].reshape(gt, 128)
                u = (u * cos + pltpu.roll(u, 64, 1) * sin).astype(BF16).reshape(2, toks, 128)
                if t == 0:
                    q_buf[pl.ds(2 * g, 2), 0:toks, h * 128:(h + 1) * 128] = u
                else:
                    kn[pl.ds(2 * g, 2), :, h * 128:(h + 1) * 128] = u
        for r in range(2):
            q_copy(2 * g + r, 0).start()
            q_copy(2 * g + r, 1).start()

    def front(g, _):
        @pl.when(g < groups)
        def _():
            project(g)

        @pl.when(g == 1)
        def _():
            w_hop(2)

        @pl.when(g == 2)
        def _():
            w_hop(3)

        @pl.when(g > 0)
        def _():
            normalize(g - 1)
        return 0

    lax.fori_loop(0, groups + 1, front, 0)

    outs = (pltpu.make_async_copy(kn, ok_hbm, out_sem.at[groups]), pltpu.make_async_copy(vn, ov_hbm, out_sem.at[groups + 1]))
    for cpy in outs:
        cpy.start()

    nw = 2 * last

    def wslice(d, c):
        return wf.at[:, pl.ds(pl.multiple_of((d * 4 + c) * piece, piece), piece), :]

    def w_copy(i):
        ref = (wslice(dp, me), wslice(dp, me), wslice(dp, me), wslice(dp, counter), wslice(dp, counter), wslice(1 - dp, me), wslice(1 - dp, counter))[i]
        dev = ({'cp': counter}, {'dp': 1 - dp}, {'cp': partner}, {'dp': 1 - dp}, {'cp': partner}, {'cp': partner}, {'cp': partner})[i]
        return remote(ref, ref, w_s.at[nw + i], w_r.at[nw + i], **dev)

    w_hop(4)
    for i in range(3):
        w_copy(i).start()

    def forward_q(b):
        q_copy(b, 1).wait_recv()
        q_copy(b, 2).start()

    forward_q(0)

    def p_copy(b, i):
        if i < 4:
            s = 1 if i < 2 else 3
            src = (q_buf.at[b, pl.ds(s * toks, toks), :], l_buf.at[b, :, pl.ds(s * toks, toks)])[i % 2]
        else:
            src = (c_o.at[b], c_l.at[b])[i % 2]
        dst = (rA.at[b], lA.at[b], rB.at[b], lB.at[b], rC.at[b], lC.at[b])[i]
        return remote(src, dst, p_s.at[b, i], p_r.at[b, i], cp=partner if i < 4 else counter)

    def blend(parts, dst):
        top = functools.reduce(jnp.maximum, [e for _, e in parts])
        ws = [jnp.exp2(e - top) for _, e in parts]
        den = functools.reduce(jnp.add, ws)
        cols = [jnp.transpose(w / den) for w in ws]
        for h in range(heads):
            hs = slice(h * 128, (h + 1) * 128)
            acc = functools.reduce(jnp.add, [c[:, h:h + 1] * v[:, hs].astype(F32) for c, (v, _) in zip(cols, parts)])
            dst[:, hs] = acc.astype(BF16)
        return top + jnp.log2(den)

    def precombine(b):
        p_copy(b, 2).wait_recv()
        p_copy(b, 3).wait_recv()
        c_l[b] = blend([(q_buf.at[b, pl.ds(2 * toks, toks), :], l_buf[b, :, 2 * toks:3 * toks]), (rB.at[b], lB[b])], c_o.at[b])
        p_copy(b, 4).start()
        p_copy(b, 5).start()

    def finish(b):
        for i in (0, 1, 4, 5):
            p_copy(b, i).wait_recv()
        blend([(q_buf.at[b, pl.ds(0, toks), :], l_buf[b, :, 0:toks]), (rA.at[b], lA[b]), (rC.at[b], lC[b])], o_all.at[z, b])
        o_hop(b, 1)

    def out_copy(g):
        return pltpu.make_async_copy(x_v.at[pl.ds(2 * g, 2)], out_hbm.at[pl.ds(2 * g, 2)], out_sem.at[g])

    def project_out(g):
        o_hop(2 * g, 4)
        o_hop(2 * g + 1, 4)

        def chunk(n, ss):
            cols = pl.ds(pl.multiple_of(n * 512, 512), 512)
            y = None
            for t in range(n_tp):
                d = jnp.dot(o_all[t, pl.ds(2 * g, 2)].reshape(gt, width), wf[t, :, cols], preferred_element_type=F32)
                y = d if y is None else y + d
            s_scr[0:gt, cols] = y
            return ss + jnp.sum(y * y, axis=1, keepdims=True)

        ss = lax.fori_loop(0, model // 512, chunk, jnp.zeros((gt, 1), F32))
        inv = lax.rsqrt(ss / model + NORM_EPS)
        for n in range(model // 512):
            cols = slice(n * 512, (n + 1) * 512)
            y = s_scr[0:gt, cols] * inv * pg_ref[0:1, cols].astype(F32)
            y = x_v[pl.ds(2 * g, 2), :, cols].reshape(gt, 512).astype(F32) + y
            x_v[pl.ds(2 * g, 2), :, cols] = y.astype(BF16).reshape(2, toks, 512)
        out_copy(g).start()

    head_lane = lax.broadcasted_iota(jnp.int32, lse_scr.shape, 1)

    def row(b, _):
        @pl.when(b < rows)
        def _():
            for cpy in kv_copies(b):
                cpy.wait()

            @pl.when(b + 1 < rows)
            def _():
                for cpy in kv_copies(b + 1):
                    cpy.start()
                forward_q(b + 1)

            split_heads(raw.at[b % 2, 0], wide, k_scr, heads, slots * heads)
            split_heads(raw.at[b % 2, 1], wide, v_scr, heads, slots * heads)
            for i in (0, 2):
                q_copy(b, i).wait_recv()
            for i in range(3):
                q_copy(b, i).wait_send()

        limit = pre_ref[jnp.minimum(b, rows - 1)] - me * slots

        def head(h, _):
            @pl.when(b < rows)
            def _():
                col = pl.ds(pl.multiple_of(h * 128, 128), 128)
                o, lse = attend_head(h, q_buf[b, :, col], k_scr, v_scr, kn[b, :, col], vn[b, :, col], s_scr, limit, bias[...], 256)
                q_buf[b, :, col] = o.astype(BF16)
                lse_scr[...] = jnp.where(head_lane == h, lse, lse_scr[...])

            @pl.when(h == 0)
            def _():
                @pl.when((b >= 1) & (b < rows + 1))
                def _():
                    precombine(b - 1)

                @pl.when((b >= 2) & (b < rows + 2))
                def _():
                    o_hop(b - 2, 2)

            @pl.when(h == 1)
            def _():
                @pl.when(b == 6)
                def _():
                    for i in (2, 4, 5, 6):
                        w_copy(i).wait_recv()

                @pl.when(b == rows + 2)
                def _():
                    project_out(groups - 1)

            @pl.when(h == 2)
            def _():
                @pl.when((b >= 2) & (b < rows + 2))
                def _():
                    o_hop(b - 2, 3)

                @pl.when((b >= 1) & (b < rows + 1))
                def _():
                    finish(b - 1)

            @pl.when(h == 3)
            def _():
                @pl.when(b == 1)
                def _():
                    w_copy(0).wait_recv()
                    w_copy(3).start()
                    w_copy(4).start()

                @pl.when(b == 4)
                def _():
                    w_copy(1).wait_recv()
                    w_copy(3).wait_recv()
                    w_copy(5).start()
                    w_copy(6).start()

                @pl.when((b >= 6) & (b < 6 + groups - 1))
                def _():
                    project_out(b - 6)
            return 0

        lax.fori_loop(0, heads, head, 0)

        @pl.when(b < rows)
        def _():
            l_buf[b] = jnp.transpose(lse_scr[...])[0:8, :]
            for i in range(4):
                p_copy(b, i).start()
        return 0

    lax.fori_loop(0, rows + 3, row, 0)

    for g in range(groups):
        out_copy(g).wait()
    for cpy in outs:
        cpy.wait()

    def sent_g(g, _):
        for i in range(1, n_tp):
            st_copy(g, i).wait_send()
        return 0

    lax.fori_loop(0, groups, sent_g, 0)

    def sent_b(b, _):
        for i in range(6):
            p_copy(b, i).wait_send()
        hop_sent(lambda o: o_all.at[o, b], lambda d, i: z_s.at[b, d * last + i], lambda d, i: z_r.at[b, d * last + i])
        return 0

    lax.fori_loop(0, rows, sent_b, 0)
    hop_sent(lambda o: wf.at[o, js, :], lambda d, i: w_s.at[d * last + i], lambda d, i: w_r.at[d * last + i])
    for i in range(7):
        w_copy(i).wait_send()


def solution(mesh):
    n_tp = mesh.shape['tp']

    def local_step(x_chunk, w_query, w_key, w_value, w_out, q_gain, k_gain, post_gain, cache_k, cache_v, prefix_len):
        rows, toks, model = x_chunk.shape
        slots, heads, dim = cache_k.shape[1:]
        width = heads * dim
        n_q = 4 * toks
        positions = prefix_len[:, None] + lax.axis_index('cp') * toks + jnp.arange(toks, dtype=jnp.int32)[None, :]
        inv_freq = ROPE_BASE ** (-(jnp.arange(dim // 2, dtype=F32) * 2.0 / dim))
        angles = positions.astype(F32)[..., None] * inv_freq
        cos, sin = jnp.cos(angles), jnp.sin(angles)
        cos = jnp.concatenate([cos, cos], axis=-1)
        sin = jnp.concatenate([-sin, sin], axis=-1)
        any_ = pl.BlockSpec(memory_space=pl.ANY)
        vm = pl.BlockSpec(memory_space=pltpu.VMEM)
        dma = pltpu.SemaphoreType.DMA
        last = n_tp - 1
        scratch = [
            pltpu.VMEM((rows, toks, model), BF16), pltpu.VMEM((3, model, width), BF16), pltpu.VMEM((n_tp, width, model), BF16),
            pltpu.VMEM((rows, n_q, width), BF16), pltpu.VMEM((rows, toks, width), BF16), pltpu.VMEM((rows, toks, width), BF16),
            pltpu.VMEM((rows, toks, width), BF16), pltpu.VMEM((rows, toks, width), BF16), pltpu.VMEM((rows, toks, width), BF16),
            pltpu.VMEM((rows, 8, toks), F32), pltpu.VMEM((rows, 8, toks), F32), pltpu.VMEM((rows, 8, toks), F32),
            pltpu.VMEM((rows, toks, width), BF16), pltpu.VMEM((rows, 8, toks), F32), pltpu.VMEM((rows, 8, n_q), F32),
            pltpu.VMEM((n_tp, rows, toks, width), BF16), pltpu.VMEM((rows // 2, n_tp, 8, 2 * toks), F32),
            pltpu.VMEM((2, 2, slots * heads, dim), BF16), pltpu.VMEM((1024, 128), F32),
            pltpu.VMEM((heads, slots, dim), BF16), pltpu.VMEM((heads, slots, dim), BF16),
            pltpu.VMEM((n_q, slots), F32), pltpu.VMEM((n_q, toks), F32), pltpu.VMEM((n_q, 128), F32),
            dma((5,)), dma((2, 2)), dma((rows // 2 + 2,)), dma((rows // 2, last)), dma((rows // 2, last)),
            dma((rows, 3)), dma((rows, 3)), dma((rows, 6)), dma((rows, 6)), dma((rows, 2 * last)), dma((rows, 2 * last)),
            dma((2 * last + 7,)), dma((2 * last + 7,)),
        ]
        flops = 2 * rows * toks * model * width * 3 + 4 * rows * n_q * slots * width + 2 * rows * toks * model * model
        out, ok, ov = pl.pallas_call(
            functools.partial(step_kernel, n_tp),
            in_specs=[pl.BlockSpec(memory_space=pltpu.SMEM)] + [any_] * 5 + [vm] * 5 + [any_] * 2,
            out_specs=[any_] * 3,
            out_shape=[jax.ShapeDtypeStruct((rows, toks, model), BF16), jax.ShapeDtypeStruct((rows, toks, width), BF16), jax.ShapeDtypeStruct((rows, toks, width), BF16)],
            scratch_shapes=scratch,
            compiler_params=pltpu.CompilerParams(collective_id=0, has_side_effects=True, vmem_limit_bytes=67043328),
            cost_estimate=pl.CostEstimate(flops=flops, bytes_accessed=4 * rows * slots * width, transcendentals=rows * n_q * slots * heads),
            name="step",
        )(prefix_len, x_chunk, w_query, w_key, w_value, w_out, q_gain.reshape(1, width), k_gain.reshape(1, width), post_gain.reshape(1, model),
          cos, sin, cache_k.reshape(rows, slots * heads, dim), cache_v.reshape(rows, slots * heads, dim))
        return out, ok.reshape(rows, toks, heads, dim), ov.reshape(rows, toks, heads, dim)

    x_spec = P('dp', 'cp', None)
    head_spec = P('dp', 'cp', 'tp', None)
    in_specs = (x_spec, P(None, 'tp'), P(None, 'tp'), P(None, 'tp'), P('tp', None), P('tp'), P('tp'), P(None), head_spec, head_spec, P('dp'))
    out_specs = (x_spec, head_spec, head_spec)
    return jax.shard_map(local_step, mesh=mesh, in_specs=in_specs, out_specs=out_specs, check_vma=False)
```

time: 798 us -> 199 us (0.25)
  waiting for transfers between devices: 408 us -> 0 us
  matrix products: 193 us -> 0 us
  Pallas kernels: 0 us -> 182 us
  other arithmetic: 99 us -> 3.95 us
  local copies, waits for them, and re-layouts: 65.7 us -> 12.9 us
  blocking collectives: 13.9 us -> 0 us
  between operations: 14 us -> 0.65 us
    psum x1 -> x0, waiting for transfers between devices: 288 us -> none  [local_step(): mixed_sum = lax.psum(mixed_part, 'tp')]
    dot_general x20 -> x0, matrix products: 193 us -> none  [the longest x4 81.7 us: block_attention(): jnp.einsum('bqkgt,btkd->bqkgd', p_cache.astype(jnp.bfloat16), cache_v, pr...]
    pallas_call x0 -> x1, Pallas kernels: none -> 182 us  [local_step(): pl.pallas_call(functools.partial(step_kernel, n_tp), in_specs=[pl.BlockSp...]
    reduce_scatter x2 -> x0, waiting for transfers between devices: 89.1 us -> none  [the longest x1 70.2 us: local_step(): lax.psum_scatter(part_num * factor[..., None], 'cp', scatter_dimension=0,...]
    reduce_sum x9 -> x0, other arithmetic: 66.4 us -> none  [the longest x8 62.2 us: block_attention(): den_sum = jnp.sum(p_cache, axis=-1) + jnp.sum(p_chunk, axis=-1)]
    unnamed x36 -> x1, local copies, waits for them, and re-layouts: 49.6 us -> 4.79 us
    pmax x1 -> x0, waiting for transfers between devices: 29.8 us -> none  [local_step(): glob_max = lax.pmax(part_max, 'cp')]
    psum x1 -> x0, blocking collectives: 13.9 us -> none  [local_step(): lax.psum(jnp.stack([jnp.sum(q_raw * q_raw, axis=-1), jnp.sum(k_raw * k_ra...]
  transfers between devices with their start and end apart: 5 -> 0, of which waited for: 4 -> 0; matrix products, arithmetic and copies ran while one was open for 5% -> 0% of each run, Pallas kernels for 0% -> 0%
where the time goes in v2:
time: 199 us
  Pallas kernels  182 us (91%)
  local copies, waits for them, and re-layouts  12.9 us (6%)
  other arithmetic  3.95 us (2%)
    pallas_call x1, Pallas kernels, local_step(): pl.pallas_call(functools.partial(step_kernel, n_tp), in_specs=[pl.BlockSp...  182 us
    unnamed x1, local copies, waits for them, and re-layouts  4.79 us

profile of v2, /device:TPU:0, one launch (start us, length us, event | category | flops | bytes accessed | tf_op | source)
XLA Modules:
  0.0 199.0 jit_solution(7137810268315270557)
XLA Ops:
  0.6 0.7 broadcast_add_fusion
  1.3 1.3 reshape.56.qg_ref
  2.6 1.3 reshape.57.kg_ref
  3.8 0.1 add_convert_fusion
  3.9 1.3 reshape.58.pg_ref
  5.2 1.9 fusion
  7.1 1.3 pad_maximum_fusion
  8.4 181.6 %step.1 = (bf16[8,128,2048]{2,1,0:T(8,128)(2,1)}, bf16[8,128,512]{2,1,0:T(8,128)(2,1)}, bf16[8,128,512]{2,1,0:T(8,128)(2,1)}) custom-call(s32[8]{0:T(128)} %pre_ref.1, bf16[8,128,2048]{2,1,0:T(8,128)(2,1)} %x_hbm.1, bf16[2048,512]{1,0:T(8,128)(2,1)} %wq_hbm.1, bf16[2048,512]{1,0:T(8,128)(2,1)} %wk_hbm.1, bf16[2048,512]{1,0:T(8,128)(2,1)} %wv_hbm.1, ...), custom_call_target="tpu_custom_call" | custom-call | flops 32212254720 | bytes 33554432 | tf_op jit(solution)/shard_map/step/pallas_call | solution.py:448
  190.0 2.1 %reshape.61 = bf16[8,128,4,128]{3,2,1,0:T(4,128)(2,1)} reshape(bf16[8,128,512]{2,1,0:T(8,128)(2,1)} %get-tuple-element.7) | data formatting | bytes 2097152 | tf_op jit(solution)/shard_map/reshape | solution.py:459
  192.1 2.1 %reshape.62 = bf16[8,128,4,128]{3,2,1,0:T(4,128)(2,1)} reshape(bf16[8,128,512]{2,1,0:T(8,128)(2,1)} %get-tuple-element.8) | data formatting | bytes 2097152 | tf_op jit(solution)/shard_map/reshape | solution.py:459
  194.2 4.8 %copy.15 = bf16[8,128,2048]{2,1,0:T(8,128)(2,1)} copy(bf16[8,128,2048]{2,1,0:T(8,128)(2,1)} %get-tuple-element.17) | data formatting | bytes 8388608
  (1 shorter events, 0.0 us)

commit v3 on v2

--- a/solution.py
+++ b/solution.py
@@ -23,39 +23,58 @@
     def body(i, _):
         wide_ref[...] = raw_ref[pl.ds(i * step, step), :].astype(F32)
         for h in range(heads):
-            out_ref[h, pl.ds(i * per, per), :] = wide_ref[pl.ds(h, per, stride=heads), :].astype(BF16)
+            out_ref[h, pl.ds(i * per, per), 0:128] = wide_ref[pl.ds(h, per, stride=heads), :].astype(BF16)
         return 0
 
     lax.fori_loop(0, rows // step, body, 0)
 
 
-def attend_head(h, q, k_ref, v_ref, kc, vc, s_ref, limit, bias, tile):
-    n_t = k_ref.shape[1] // tile
-    lane = lax.broadcasted_iota(jnp.int32, (1, tile), 1)
-    s_c = lax.dot_general(q, kc, NT, preferred_element_type=F32)
-    s_c = jnp.where(bias >= 0, s_c, MASK_VALUE)
-    mx = s_c
+SCALE = (128 ** -0.5) * LOG2E
+TILE = 256
+
+
+def scores(q, h, kc, bias, k_ref, s_ref, limit):
+    n_t = k_ref.shape[1] // TILE
+    lane = lax.broadcasted_iota(jnp.int32, (1, TILE), 1)
+    s = lax.dot_general(q, kc, NT, preferred_element_type=F32)
+    s = jnp.where(bias >= 0, s, MASK_VALUE)
+    s_ref[:, n_t * TILE:n_t * TILE + 128] = s
+    mx = s
     for j in range(n_t):
-        s = lax.dot_general(q, k_ref[h, j * tile:(j + 1) * tile, :], NT, preferred_element_type=F32)
-        s = jnp.where(lane + j * tile < limit, s, MASK_VALUE)
-        s_ref[:, j * tile:(j + 1) * tile] = s
-        for u in range(tile // 128):
+        s = lax.dot_general(q, k_ref[h, j * TILE:(j + 1) * TILE, :], NT, preferred_element_type=F32)
+        s = jnp.where(lane + j * TILE < limit, s, MASK_VALUE)
+        s_ref[:, j * TILE:(j + 1) * TILE] = s
+        for u in range(TILE // 128):
             mx = jnp.maximum(mx, s[:, u * 128:(u + 1) * 128])
-    c = (128 ** -0.5) * LOG2E
-    m = jnp.max(mx, axis=1, keepdims=True)
-    p = jnp.exp2((s_c - m) * c)
-    l = p
-    acc = jnp.dot(p.astype(BF16), vc, preferred_element_type=F32)
+    return jnp.max(mx, axis=1, keepdims=True) * SCALE
+
+
+def weigh(top, h, vc, v_ref, s_ref):
+    n_t = v_ref.shape[1] // TILE
+    acc = None
     for j in range(n_t):
-        p = jnp.exp2((s_ref[:, j * tile:(j + 1) * tile] - m) * c)
-        for u in range(tile // 128):
-            l = l + p[:, u * 128:(u + 1) * 128]
-        acc = acc + jnp.dot(p.astype(BF16), v_ref[h, j * tile:(j + 1) * tile, :], preferred_element_type=F32)
-    l = jnp.sum(l, axis=1, keepdims=True)
-    return acc * (1.0 / l), m * c + jnp.log2(l)
-
-
-def step_kernel(n_tp, pre_ref, x_hbm, wq_hbm, wk_hbm, wv_hbm, wo_hbm, qg_ref, kg_ref, pg_ref, cos_ref, sin_ref, ck_hbm, cv_hbm,
+        p = jnp.exp2(s_ref[:, j * TILE:(j + 1) * TILE] * SCALE - top)
+        d = jnp.dot(p.astype(BF16), v_ref[h, j * TILE:(j + 1) * TILE, :], preferred_element_type=F32)
+        acc = d if acc is None else acc + d
+    p = jnp.exp2(s_ref[:, n_t * TILE:n_t * TILE + 128] * SCALE - top)
+    return acc + jnp.dot(p.astype(BF16), vc, preferred_element_type=F32)
+
+
+def attend_head(h, q_ref, kc, vc, k_ref, v_ref, s_ref, limit, bias_ref, lse_ref):
+    col = pl.ds(pl.multiple_of(h * 128, 128), 128)
+    half = q_ref.shape[0] // 2
+    vc = jnp.concatenate([vc, jnp.ones(vc.shape, BF16)], axis=1)
+    parts = [slice(r * half, (r + 1) * half) for r in range(2)]
+    tops = [scores(q_ref[rs, col], h, kc, bias_ref[rs, :], k_ref, s_ref.at[rs], limit) for rs in parts]
+    lane = lax.broadcasted_iota(jnp.int32, (half, 128), 1)
+    for rs, top in zip(parts, tops):
+        acc = weigh(top, h, vc, v_ref, s_ref.at[rs])
+        den = acc[:, 128:]
+        q_ref[rs, col] = (acc[:, :128] * (1.0 / den)).astype(BF16)
+        lse_ref[rs, :] = jnp.where(lane == h, top + jnp.log2(den), lse_ref[rs, :])
+
+
+def step_kernel(n_tp, pre_ref, x_hbm, wq_hbm, wk_hbm, wv_hbm, wo_hbm, gain_ref, cos_ref, sin_ref, ck_hbm, cv_hbm,
                 out_hbm, ok_hbm, ov_hbm,
                 x_v, wqkv, wf, q_buf, kn, vn, rA, rB, rC, lA, lB, lC, c_o, c_l, l_buf, o_all, st,
                 raw, wide, k_scr, v_scr, s_scr, bias, lse_scr,
@@ -142,6 +161,7 @@
     for s, blk in enumerate((me, partner, counter, diag)):
         bias[s * toks:(s + 1) * toks, :] = jnp.where(ki - qi <= (blk - me) * toks, 0.0, -1.0)
     lse_scr[...] = jnp.zeros(lse_scr.shape, F32)
+    v_scr[:, :, 128:] = jnp.ones((heads, slots, 128), BF16)
 
     for cpy in loads:
         cpy.wait()
@@ -178,10 +198,10 @@
         for i in range(1, n_tp):
             tot = tot + st[g, i]
         inv = jnp.transpose(lax.rsqrt(tot / (width * n_tp) + NORM_EPS))
-        for t, (gain, base) in enumerate(((qg_ref, 0), (kg_ref, gt))):
+        for t, (gain, base) in enumerate(((0, 0), (width, gt))):
             for h in range(heads):
                 u = s_scr[base:base + gt, pl.ds(pl.multiple_of(g * width + h * 128, 128), 128)]
-                u = u * inv[:, t:t + 1] * gain[0:1, h * 128:(h + 1) * 128].astype(F32)
+                u = u * inv[:, t:t + 1] * gain_ref[0:1, gain + h * 128:gain + (h + 1) * 128]
                 cos = cos_ref[pl.ds(2 * g, 2)].reshape(gt, 128)
                 sin = sin_ref[pl.ds(2 * g, 2)].reshape(gt, 128)
                 u = (u * cos + pltpu.roll(u, 64, 1) * sin).astype(BF16).reshape(2, toks, 128)
@@ -290,12 +310,10 @@
         inv = lax.rsqrt(ss / model + NORM_EPS)
         for n in range(model // 512):
             cols = slice(n * 512, (n + 1) * 512)
-            y = s_scr[0:gt, cols] * inv * pg_ref[0:1, cols].astype(F32)
+            y = s_scr[0:gt, cols] * inv * gain_ref[0:1, 2 * width + n * 512:2 * width + (n + 1) * 512]
             y = x_v[pl.ds(2 * g, 2), :, cols].reshape(gt, 512).astype(F32) + y
             x_v[pl.ds(2 * g, 2), :, cols] = y.astype(BF16).reshape(2, toks, 512)
         out_copy(g).start()
-
-    head_lane = lax.broadcasted_iota(jnp.int32, lse_scr.shape, 1)
 
     def row(b, _):
         @pl.when(b < rows)
@@ -322,9 +340,7 @@
             @pl.when(b < rows)
             def _():
                 col = pl.ds(pl.multiple_of(h * 128, 128), 128)
-                o, lse = attend_head(h, q_buf[b, :, col], k_scr, v_scr, kn[b, :, col], vn[b, :, col], s_scr, limit, bias[...], 256)
-                q_buf[b, :, col] = o.astype(BF16)
-                lse_scr[...] = jnp.where(head_lane == h, lse, lse_scr[...])
+                attend_head(h, q_buf.at[b], kn[b, :, col], vn[b, :, col], k_scr, v_scr, s_scr, limit, bias, lse_scr)
 
             @pl.when(h == 0)
             def _():
@@ -438,8 +454,8 @@
             pltpu.VMEM((rows, toks, width), BF16), pltpu.VMEM((rows, 8, toks), F32), pltpu.VMEM((rows, 8, n_q), F32),
             pltpu.VMEM((n_tp, rows, toks, width), BF16), pltpu.VMEM((rows // 2, n_tp, 8, 2 * toks), F32),
             pltpu.VMEM((2, 2, slots * heads, dim), BF16), pltpu.VMEM((1024, 128), F32),
-            pltpu.VMEM((heads, slots, dim), BF16), pltpu.VMEM((heads, slots, dim), BF16),
-            pltpu.VMEM((n_q, slots), F32), pltpu.VMEM((n_q, toks), F32), pltpu.VMEM((n_q, 128), F32),
+            pltpu.VMEM((heads, slots, dim), BF16), pltpu.VMEM((heads, slots, 2 * dim), BF16),
+            pltpu.VMEM((n_q, slots + toks), F32), pltpu.VMEM((n_q, toks), F32), pltpu.VMEM((n_q, 128), F32),
             dma((5,)), dma((2, 2)), dma((rows // 2 + 2,)), dma((rows // 2, last)), dma((rows // 2, last)),
             dma((rows, 3)), dma((rows, 3)), dma((rows, 6)), dma((rows, 6)), dma((rows, 2 * last)), dma((rows, 2 * last)),
             dma((2 * last + 7,)), dma((2 * last + 7,)),
@@ -447,14 +463,14 @@
         flops = 2 * rows * toks * model * width * 3 + 4 * rows * n_q * slots * width + 2 * rows * toks * model * model
         out, ok, ov = pl.pallas_call(
             functools.partial(step_kernel, n_tp),
-            in_specs=[pl.BlockSpec(memory_space=pltpu.SMEM)] + [any_] * 5 + [vm] * 5 + [any_] * 2,
+            in_specs=[pl.BlockSpec(memory_space=pltpu.SMEM)] + [any_] * 5 + [vm] * 3 + [any_] * 2,
             out_specs=[any_] * 3,
             out_shape=[jax.ShapeDtypeStruct((rows, toks, model), BF16), jax.ShapeDtypeStruct((rows, toks, width), BF16), jax.ShapeDtypeStruct((rows, toks, width), BF16)],
             scratch_shapes=scratch,
             compiler_params=pltpu.CompilerParams(collective_id=0, has_side_effects=True, vmem_limit_bytes=67043328),
             cost_estimate=pl.CostEstimate(flops=flops, bytes_accessed=4 * rows * slots * width, transcendentals=rows * n_q * slots * heads),
             name="step",
-        )(prefix_len, x_chunk, w_query, w_key, w_value, w_out, q_gain.reshape(1, width), k_gain.reshape(1, width), post_gain.reshape(1, model),
+        )(prefix_len, x_chunk, w_query, w_key, w_value, w_out, jnp.concatenate([q_gain, k_gain, post_gain]).astype(F32).reshape(1, 2 * width + model),
           cos, sin, cache_k.reshape(rows, slots * heads, dim), cache_v.reshape(rows, slots * heads, dim))
         return out, ok.reshape(rows, toks, heads, dim), ov.reshape(rows, toks, heads, dim)
 

time: 199 us -> 178 us (0.89)
  Pallas kernels: 182 us -> 161 us
    pallas_call x1, Pallas kernels: 182 us -> 161 us  [local_step(): pl.pallas_call(functools.partial(step_kernel, n_tp), in_specs=[pl.BlockSp...]
    reshape x3 -> x0, local copies, waits for them, and re-layouts: 3.82 us -> none  [the longest x1 1.29 us: local_step(): post_gain.reshape(1, model)]
    concatenate x0 -> x3, local copies, waits for them, and re-layouts: none -> 2.06 us  [local_step(): jnp.concatenate([q_gain, k_gain, post_gain]).astype(F32)]
where the time goes in v3:
time: 178 us; the launch traced here: 177 us
  Pallas kernels  161 us (90%)
  local copies, waits for them, and re-layouts  11.1 us (6%)
  other arithmetic  4.56 us (3%)
    pallas_call x1, Pallas kernels, local_step(): pl.pallas_call(functools.partial(step_kernel, n_tp), in_specs=[pl.BlockSp...  161 us
    unnamed x1, local copies, waits for them, and re-layouts  4.79 us

profile of v3, /device:TPU:0, one launch (start us, length us, event | category | flops | bytes accessed | tf_op | source)
XLA Modules:
  0.0 177.2 jit_solution(8909277051375945697)
XLA Ops:
  0.6 0.7 broadcast_add_fusion
  1.3 0.7 concatenate.22
  2.0 0.7 concatenate.23
  2.7 0.1 add_convert_fusion
  2.7 0.7 concatenate.24
  3.4 0.6 maximum_convert_fusion.gain_ref
  4.1 1.9 %fusion = (f32[8,128,64]{2,1,0:T(8,128)S(1)}, f32[8,128,64]{2,1,0:T(8,128)S(1)}, f32[8,128,64]{2,1,0:T(8,128)S(1)}) fusion(f32[64]{0:T(128)S(1)} %negate_power_fusion, f32[8,128]{1,0:T(8,128)S(1)} %add_convert_fusion), kind=kLoop, calls=%fused_computation.4 | loop fusion | flops 131072 | bytes 790784 | tf_op jit(solution)/shard_map/neg | solution.py:444
  6.0 1.3 pad_maximum_fusion
  7.3 160.9 %step.1 = (bf16[8,128,2048]{2,1,0:T(8,128)(2,1)}, bf16[8,128,512]{2,1,0:T(8,128)(2,1)}, bf16[8,128,512]{2,1,0:T(8,128)(2,1)}) custom-call(s32[8]{0:T(128)} %pre_ref.1, bf16[8,128,2048]{2,1,0:T(8,128)(2,1)} %x_hbm.1, bf16[2048,512]{1,0:T(8,128)(2,1)} %wq_hbm.1, bf16[2048,512]{1,0:T(8,128)(2,1)} %wk_hbm.1, bf16[2048,512]{1,0:T(8,128)(2,1)} %wv_hbm.1, ...), custom_call_target="tpu_custom_call" | custom-call | flops 32212254720 | bytes 33554432 | tf_op jit(solution)/shard_map/step/pallas_call | solution.py:464
  168.2 2.1 %reshape.92 = bf16[8,128,4,128]{3,2,1,0:T(4,128)(2,1)} reshape(bf16[8,128,512]{2,1,0:T(8,128)(2,1)} %get-tuple-element.7) | data formatting | bytes 2097152 | tf_op jit(solution)/shard_map/reshape | solution.py:475
  170.3 2.1 %reshape.93 = bf16[8,128,4,128]{3,2,1,0:T(4,128)(2,1)} reshape(bf16[8,128,512]{2,1,0:T(8,128)(2,1)} %get-tuple-element.8) | data formatting | bytes 2097152 | tf_op jit(solution)/shard_map/reshape | solution.py:475
  172.5 4.8 %copy.15 = bf16[8,128,2048]{2,1,0:T(8,128)(2,1)} copy(bf16[8,128,2048]{2,1,0:T(8,128)(2,1)} %get-tuple-element.17) | data formatting | bytes 8388608
  (1 shorter events, 0.0 us)

commit v4 on v3

--- a/solution.py
+++ b/solution.py
@@ -94,14 +94,19 @@
     def remote(src, dst, ss, rs, **dev):
         return pltpu.make_async_remote_copy(src_ref=src, dst_ref=dst, send_sem=ss, recv_sem=rs, device_id=dev, device_id_type=MESH)
 
-    loads = [pltpu.make_async_copy(x_hbm, x_v, in_sem.at[0])]
-    for i, w in enumerate((wq_hbm, wk_hbm, wv_hbm)):
-        loads.append(pltpu.make_async_copy(w, wqkv.at[i], in_sem.at[1 + i]))
+    def x_copy(g):
+        return pltpu.make_async_copy(x_hbm.at[pl.ds(2 * g, 2)], x_v.at[pl.ds(2 * g, 2)], in_sem.at[4 + g])
+
+    w_copies = [pltpu.make_async_copy(w, wqkv.at[i], in_sem.at[1 + i]) for i, w in enumerate((wq_hbm, wk_hbm, wv_hbm))]
     js = pl.ds(pl.multiple_of((dp * 4 + me) * piece, piece), piece)
-    w_local = pltpu.make_async_copy(wo_hbm.at[js, :], wf.at[z, js, :], in_sem.at[4])
+    w_local = pltpu.make_async_copy(wo_hbm.at[js, :], wf.at[z, js, :], in_sem.at[0])
+    w_copies[0].start()
+    x_copy(0).start()
     w_local.start()
-    for cpy in loads:
-        cpy.start()
+    w_copies[1].start()
+    w_copies[2].start()
+    for g in range(1, groups):
+        x_copy(g).start()
 
     def kv_copies(b):
         par = b % 2
@@ -163,9 +168,6 @@
     lse_scr[...] = jnp.zeros(lse_scr.shape, F32)
     v_scr[:, :, 128:] = jnp.ones((heads, slots, 128), BF16)
 
-    for cpy in loads:
-        cpy.wait()
-
     def st_copy(g, i):
         return remote(st.at[g, 0], st.at[g, i], st_s.at[g, i - 1], st_r.at[g, i - 1], tp=(z + i) % n_tp)
 
@@ -175,10 +177,20 @@
         return remote(src, dst, q_s.at[b, i], q_r.at[b, i], cp=counter if i == 1 else partner)
 
     def project(g):
+        x_copy(g).wait()
+
+        @pl.when(g == 0)
+        def _():
+            w_copies[0].wait()
         xg = x_v[pl.ds(2 * g, 2)].reshape(gt, model)
         cols = pl.ds(pl.multiple_of(g * width, width), width)
         q = jnp.dot(xg, wqkv[0], preferred_element_type=F32)
         s_scr[0:gt, cols] = q
+
+        @pl.when(g == 0)
+        def _():
+            w_copies[1].wait()
+            w_copies[2].wait()
         k = jnp.dot(xg, wqkv[1], preferred_element_type=F32)
         s_scr[gt:2 * gt, cols] = k
         lane = lax.broadcasted_iota(jnp.int32, (gt, 128), 1)
@@ -218,14 +230,6 @@
         def _():
             project(g)
 
-        @pl.when(g == 1)
-        def _():
-            w_hop(2)
-
-        @pl.when(g == 2)
-        def _():
-            w_hop(3)
-
         @pl.when(g > 0)
         def _():
             normalize(g - 1)
@@ -240,16 +244,30 @@
     nw = 2 * last
 
     def wslice(d, c):
-        return wf.at[:, pl.ds(pl.multiple_of((d * 4 + c) * piece, piece), piece), :]
-
-    def w_copy(i):
-        ref = (wslice(dp, me), wslice(dp, me), wslice(dp, me), wslice(dp, counter), wslice(dp, counter), wslice(1 - dp, me), wslice(1 - dp, counter))[i]
-        dev = ({'cp': counter}, {'dp': 1 - dp}, {'cp': partner}, {'dp': 1 - dp}, {'cp': partner}, {'cp': partner}, {'cp': partner})[i]
-        return remote(ref, ref, w_s.at[nw + i], w_r.at[nw + i], **dev)
-
-    w_hop(4)
-    for i in range(3):
-        w_copy(i).start()
+        return pl.ds(pl.multiple_of((d * 4 + c) * piece, piece), piece)
+
+    def w_send(k, t, ref, **dev):
+        return remote(ref, ref, w_s.at[nw + k + t], w_r.at[nw + k + t], **dev)
+
+    def w_y(t):
+        return w_send(0, t, wf.at[t, wslice(dp, me), :], cp=counter)
+
+    def w_x_own():
+        return w_send(n_tp, 0, wf.at[:, wslice(dp, me), :], dp=1 - dp)
+
+    def w_d_own():
+        return w_send(n_tp, 1, wf.at[:, wslice(dp, me), :], cp=partner)
+
+    def w_x_fwd(t):
+        return w_send(n_tp + 2, t, wf.at[t, wslice(dp, counter), :], dp=1 - dp)
+
+    def w_d_fwd(t):
+        return w_send(2 * n_tp + 2, t, wf.at[t, wslice(dp, counter), :], cp=partner)
+
+    def w_d_far(i):
+        return w_send(3 * n_tp + 2, i, wf.at[:, wslice(1 - dp, (me, counter)[i]), :], cp=partner)
+
+    w_hop(2)
 
     def forward_q(b):
         q_copy(b, 1).wait_recv()
@@ -348,20 +366,33 @@
                 def _():
                     precombine(b - 1)
 
+                @pl.when((b >= 1) & (b < 1 + n_tp))
+                def _():
+                    w_y(b - 1).start()
+
+                @pl.when((b >= 2) & (b < 2 + n_tp))
+                def _():
+                    w_y(b - 2).wait_recv()
+                    w_x_fwd(b - 2).start()
+                    w_d_fwd(b - 2).start()
+
                 @pl.when((b >= 2) & (b < rows + 2))
                 def _():
                     o_hop(b - 2, 2)
 
             @pl.when(h == 1)
             def _():
-                @pl.when(b == 6)
-                def _():
-                    for i in (2, 4, 5, 6):
-                        w_copy(i).wait_recv()
-
-                @pl.when(b == rows + 2)
-                def _():
-                    project_out(groups - 1)
+                @pl.when(b == 0)
+                def _():
+                    w_hop(3)
+
+                @pl.when(b == rows)
+                def _():
+                    w_d_own().wait_recv()
+                    for t in range(n_tp):
+                        w_d_fwd(t).wait_recv()
+                    for i in range(2):
+                        w_d_far(i).wait_recv()
 
             @pl.when(h == 2)
             def _():
@@ -375,22 +406,25 @@
 
             @pl.when(h == 3)
             def _():
-                @pl.when(b == 1)
-                def _():
-                    w_copy(0).wait_recv()
-                    w_copy(3).start()
-                    w_copy(4).start()
-
-                @pl.when(b == 4)
-                def _():
-                    w_copy(1).wait_recv()
-                    w_copy(3).wait_recv()
-                    w_copy(5).start()
-                    w_copy(6).start()
-
-                @pl.when((b >= 6) & (b < 6 + groups - 1))
-                def _():
-                    project_out(b - 6)
+                @pl.when(b == 0)
+                def _():
+                    w_hop(4)
+                    w_x_own().start()
+                    w_d_own().start()
+
+                @pl.when(b == rows - 1)
+                def _():
+                    w_x_own().wait_recv()
+                    for t in range(n_tp):
+                        w_x_fwd(t).wait_recv()
+                    for i in range(2):
+                        w_d_far(i).start()
+
+            turn = b * heads + h - (rows * heads + 1)
+
+            @pl.when((turn >= 0) & (turn % 2 == 0) & (turn < 2 * groups - 2) | (turn == 2 * groups))
+            def _():
+                project_out(jnp.minimum(turn // 2, groups - 1))
             return 0
 
         lax.fori_loop(0, heads, head, 0)
@@ -424,8 +458,14 @@
 
     lax.fori_loop(0, rows, sent_b, 0)
     hop_sent(lambda o: wf.at[o, js, :], lambda d, i: w_s.at[d * last + i], lambda d, i: w_r.at[d * last + i])
-    for i in range(7):
-        w_copy(i).wait_send()
+    w_x_own().wait_send()
+    w_d_own().wait_send()
+    for t in range(n_tp):
+        w_y(t).wait_send()
+        w_x_fwd(t).wait_send()
+        w_d_fwd(t).wait_send()
+    for i in range(2):
+        w_d_far(i).wait_send()
 
 
 def solution(mesh):
@@ -456,9 +496,9 @@
             pltpu.VMEM((2, 2, slots * heads, dim), BF16), pltpu.VMEM((1024, 128), F32),
             pltpu.VMEM((heads, slots, dim), BF16), pltpu.VMEM((heads, slots, 2 * dim), BF16),
             pltpu.VMEM((n_q, slots + toks), F32), pltpu.VMEM((n_q, toks), F32), pltpu.VMEM((n_q, 128), F32),
-            dma((5,)), dma((2, 2)), dma((rows // 2 + 2,)), dma((rows // 2, last)), dma((rows // 2, last)),
+            dma((4 + rows // 2,)), dma((2, 2)), dma((rows // 2 + 2,)), dma((rows // 2, last)), dma((rows // 2, last)),
             dma((rows, 3)), dma((rows, 3)), dma((rows, 6)), dma((rows, 6)), dma((rows, 2 * last)), dma((rows, 2 * last)),
-            dma((2 * last + 7,)), dma((2 * last + 7,)),
+            dma((2 * last + 3 * n_tp + 4,)), dma((2 * last + 3 * n_tp + 4,)),
         ]
         flops = 2 * rows * toks * model * width * 3 + 4 * rows * n_q * slots * width + 2 * rows * toks * model * model
         out, ok, ov = pl.pallas_call(

time: 178 us -> 155 us (0.87)
  Pallas kernels: 161 us -> 138 us
    pallas_call x1, Pallas kernels: 161 us -> 138 us  [local_step(): pl.pallas_call(functools.partial(step_kernel, n_tp), in_specs=[pl.BlockSp...]
where the time goes in v4:
time: 155 us
  Pallas kernels  138 us (89%)
  local copies, waits for them, and re-layouts  11.1 us (7%)
  other arithmetic  4.56 us (3%)
    pallas_call x1, Pallas kernels, local_step(): pl.pallas_call(functools.partial(step_kernel, n_tp), in_specs=[pl.BlockSp...  138 us
    unnamed x1, local copies, waits for them, and re-layouts  4.79 us

profile of v4, /device:TPU:0, one launch (start us, length us, event | category | flops | bytes accessed | tf_op | source)
XLA Modules:
  0.0 154.7 jit_solution(7918679022588896696)
XLA Ops:
  0.6 0.7 broadcast_add_fusion
  1.3 0.7 concatenate.22
  2.0 0.7 concatenate.23
  2.7 0.1 add_convert_fusion
  2.7 0.7 concatenate.24
  3.4 0.6 maximum_convert_fusion.gain_ref
  4.1 1.9 %fusion = (f32[8,128,64]{2,1,0:T(8,128)S(1)}, f32[8,128,64]{2,1,0:T(8,128)S(1)}, f32[8,128,64]{2,1,0:T(8,128)S(1)}) fusion(f32[64]{0:T(128)S(1)} %negate_power_fusion, f32[8,128]{1,0:T(8,128)S(1)} %add_convert_fusion), kind=kLoop, calls=%fused_computation.4 | loop fusion | flops 131072 | bytes 790784 | tf_op jit(solution)/shard_map/neg | solution.py:484
  6.0 1.3 pad_maximum_fusion
  7.3 138.4 %step.1 = (bf16[8,128,2048]{2,1,0:T(8,128)(2,1)}, bf16[8,128,512]{2,1,0:T(8,128)(2,1)}, bf16[8,128,512]{2,1,0:T(8,128)(2,1)}) custom-call(s32[8]{0:T(128)} %pre_ref.1, bf16[8,128,2048]{2,1,0:T(8,128)(2,1)} %x_hbm.1, bf16[2048,512]{1,0:T(8,128)(2,1)} %wq_hbm.1, bf16[2048,512]{1,0:T(8,128)(2,1)} %wk_hbm.1, bf16[2048,512]{1,0:T(8,128)(2,1)} %wv_hbm.1, ...), custom_call_target="tpu_custom_call" | custom-call | flops 32212254720 | bytes 33554432 | tf_op jit(solution)/shard_map/step/pallas_call | solution.py:504
  145.6 2.1 %reshape.92 = bf16[8,128,4,128]{3,2,1,0:T(4,128)(2,1)} reshape(bf16[8,128,512]{2,1,0:T(8,128)(2,1)} %get-tuple-element.7) | data formatting | bytes 2097152 | tf_op jit(solution)/shard_map/reshape | solution.py:515
  147.8 2.1 %reshape.93 = bf16[8,128,4,128]{3,2,1,0:T(4,128)(2,1)} reshape(bf16[8,128,512]{2,1,0:T(8,128)(2,1)} %get-tuple-element.8) | data formatting | bytes 2097152 | tf_op jit(solution)/shard_map/reshape | solution.py:515
  149.9 4.8 %copy.15 = bf16[8,128,2048]{2,1,0:T(8,128)(2,1)} copy(bf16[8,128,2048]{2,1,0:T(8,128)(2,1)} %get-tuple-element.17) | data formatting | bytes 8388608
  (1 shorter events, 0.0 us)

commit v5 on v4

--- a/solution.py
+++ b/solution.py
@@ -237,9 +237,23 @@
 
     lax.fori_loop(0, groups + 1, front, 0)
 
-    outs = (pltpu.make_async_copy(kn, ok_hbm, out_sem.at[groups]), pltpu.make_async_copy(vn, ov_hbm, out_sem.at[groups + 1]))
-    for cpy in outs:
-        cpy.start()
+    n_out = rows * toks * heads
+    outs = [pltpu.make_async_copy(raw.at[0, i, pl.ds(0, n_out), :], dst, out_sem.at[groups + i]) for i, dst in enumerate((ok_hbm, ov_hbm))]
+
+    def interleave():
+        per = toks * heads
+
+        def one(r, _):
+            for i, src in enumerate((kn, vn)):
+                for h in range(heads):
+                    wide[pl.ds(i * per + h, toks, stride=heads), :] = src[r, :, h * 128:(h + 1) * 128].astype(F32)
+            for i in range(2):
+                raw[0, i, pl.ds(pl.multiple_of(r * per, per), per), :] = wide[i * per:(i + 1) * per, :].astype(BF16)
+            return 0
+
+        lax.fori_loop(0, rows, one, 0)
+        for cpy in outs:
+            cpy.start()
 
     nw = 2 * last
 
@@ -376,12 +390,20 @@
                     w_x_fwd(b - 2).start()
                     w_d_fwd(b - 2).start()
 
+                @pl.when((b >= 3) & (b < rows + 3))
+                def _():
+                    o_hop(b - 3, 3)
+
+                @pl.when(b == rows + 2)
+                def _():
+                    interleave()
+
+            @pl.when(h == 1)
+            def _():
                 @pl.when((b >= 2) & (b < rows + 2))
                 def _():
                     o_hop(b - 2, 2)
 
-            @pl.when(h == 1)
-            def _():
                 @pl.when(b == 0)
                 def _():
                     w_hop(3)
@@ -396,10 +418,6 @@
 
             @pl.when(h == 2)
             def _():
-                @pl.when((b >= 2) & (b < rows + 2))
-                def _():
-                    o_hop(b - 2, 3)
-
                 @pl.when((b >= 1) & (b < rows + 1))
                 def _():
                     finish(b - 1)
@@ -466,6 +484,33 @@
         w_d_fwd(t).wait_send()
     for i in range(2):
         w_d_far(i).wait_send()
+
+
+def settle_kernel(n, *refs):
+    srcs, dsts, bufs, in_sem, out_sem = refs[:n], refs[n:2 * n], refs[2 * n:3 * n], refs[3 * n], refs[3 * n + 1]
+    jobs = []
+    for i, (s, d, v) in enumerate(zip(srcs, dsts, bufs)):
+        step = s.shape[0] // 8
+        for c in range(8):
+            rs = pl.ds(c * step, step)
+            jobs.append((pltpu.make_async_copy(s.at[rs], v.at[rs], in_sem.at[i, c]), pltpu.make_async_copy(v.at[rs], d.at[rs], out_sem.at[i, c])))
+    for a, _ in jobs:
+        a.start()
+    for a, o in jobs:
+        a.wait()
+        o.start()
+    for _, o in jobs:
+        o.wait()
+
+
+def settle(arrays):
+    n = len(arrays)
+    any_ = pl.BlockSpec(memory_space=pl.ANY)
+    return pl.pallas_call(
+        functools.partial(settle_kernel, n), in_specs=[any_] * n, out_specs=[any_] * n,
+        out_shape=[jax.ShapeDtypeStruct(a.shape, a.dtype) for a in arrays],
+        scratch_shapes=[pltpu.VMEM(a.shape, a.dtype) for a in arrays] + [pltpu.SemaphoreType.DMA((n, 8)), pltpu.SemaphoreType.DMA((n, 8))],
+        name="settle")(*arrays)
 
 
 def solution(mesh):
@@ -505,13 +550,14 @@
             functools.partial(step_kernel, n_tp),
             in_specs=[pl.BlockSpec(memory_space=pltpu.SMEM)] + [any_] * 5 + [vm] * 3 + [any_] * 2,
             out_specs=[any_] * 3,
-            out_shape=[jax.ShapeDtypeStruct((rows, toks, model), BF16), jax.ShapeDtypeStruct((rows, toks, width), BF16), jax.ShapeDtypeStruct((rows, toks, width), BF16)],
+            out_shape=[jax.ShapeDtypeStruct((rows, toks, model), BF16), jax.ShapeDtypeStruct((rows * toks * heads, dim), BF16), jax.ShapeDtypeStruct((rows * toks * heads, dim), BF16)],
             scratch_shapes=scratch,
             compiler_params=pltpu.CompilerParams(collective_id=0, has_side_effects=True, vmem_limit_bytes=67043328),
             cost_estimate=pl.CostEstimate(flops=flops, bytes_accessed=4 * rows * slots * width, transcendentals=rows * n_q * slots * heads),
             name="step",
         )(prefix_len, x_chunk, w_query, w_key, w_value, w_out, jnp.concatenate([q_gain, k_gain, post_gain]).astype(F32).reshape(1, 2 * width + model),
           cos, sin, cache_k.reshape(rows, slots * heads, dim), cache_v.reshape(rows, slots * heads, dim))
+        out, ok, ov = settle((out, ok, ov))
         return out, ok.reshape(rows, toks, heads, dim), ov.reshape(rows, toks, heads, dim)
 
     x_spec = P('dp', 'cp', None)

time: 155 us -> 151 us (0.974)
  local copies, waits for them, and re-layouts: 11.1 us -> 2.06 us
  Pallas kernels: 138 us -> 144 us
    pallas_call x0 -> x1, Pallas kernels: none -> 5.64 us  [settle(): pl.pallas_call(functools.partial(settle_kernel, n), in_specs=[any_] * n,...]
    unnamed x1 -> x0, local copies, waits for them, and re-layouts: 4.79 us -> none
    reshape x2 -> x0, local copies, waits for them, and re-layouts: 4.27 us -> none  [the longest x1 2.14 us: local_step(): ok.reshape(rows, toks, heads, dim)]
where the time goes in v5:
time: 151 us
  Pallas kernels  144 us (95%)
  other arithmetic  4.56 us (3%)
  local copies, waits for them, and re-layouts  2.06 us (1%)
    pallas_call x1, Pallas kernels, local_step(): pl.pallas_call(functools.partial(step_kernel, n_tp), in_specs=[pl.BlockSp...  138 us
    pallas_call x1, Pallas kernels, settle(): pl.pallas_call(functools.partial(settle_kernel, n), in_specs=[any_] * n,...  5.64 us

profile of v5, /device:TPU:0, one launch (start us, length us, event | category | flops | bytes accessed | tf_op | source)
XLA Modules:
  0.0 151.2 jit_solution(1431518680829807623)
XLA Ops:
  0.6 0.7 broadcast_add_fusion
  1.3 0.7 concatenate.22
  2.0 0.7 concatenate.23
  2.7 0.1 add_convert_fusion
  2.7 0.7 concatenate.24
  3.4 0.6 maximum_convert_fusion.gain_ref
  4.1 1.9 %fusion = (f32[8,128,64]{2,1,0:T(8,128)S(1)}, f32[8,128,64]{2,1,0:T(8,128)S(1)}, f32[8,128,64]{2,1,0:T(8,128)S(1)}) fusion(f32[64]{0:T(128)S(1)} %negate_power_fusion, f32[8,128]{1,0:T(8,128)S(1)} %add_convert_fusion), kind=kLoop, calls=%fused_computation.4 | loop fusion | flops 131072 | bytes 790784 | tf_op jit(solution)/shard_map/neg | solution.py:529
  6.0 1.3 pad_maximum_fusion
  7.3 138.3 %step.1 = (bf16[8,128,2048]{2,1,0:T(8,128)(2,1)}, bf16[4096,128]{1,0:T(8,128)(2,1)}, bf16[4096,128]{1,0:T(8,128)(2,1)}) custom-call(s32[8]{0:T(128)} %pre_ref.1, bf16[8,128,2048]{2,1,0:T(8,128)(2,1)} %x_hbm.1, bf16[2048,512]{1,0:T(8,128)(2,1)} %wq_hbm.1, bf16[2048,512]{1,0:T(8,128)(2,1)} %wk_hbm.1, bf16[2048,512]{1,0:T(8,128)(2,1)} %wv_hbm.1, ...), custom_call_target="tpu_custom_call" | custom-call | flops 32212254720 | bytes 33554432 | tf_op jit(solution)/shard_map/step/pallas_call | solution.py:549
  145.5 5.6 %settle.1 = (bf16[8,128,2048]{2,1,0:T(8,128)(2,1)}, bf16[4096,128]{1,0:T(8,128)(2,1)}, bf16[4096,128]{1,0:T(8,128)(2,1)}) custom-call(bf16[8,128,2048]{2,1,0:T(8,128)(2,1)} %get-tuple-element.9.refs_0_, bf16[4096,128]{1,0:T(8,128)(2,1)} %get-tuple-element.10.refs_1_, bf16[4096,128]{1,0:T(8,128)(2,1)} %get-tuple-element.11.refs_2_), custom_call_target="tpu_custom_call" | custom-call | tf_op jit(solution)/shard_map/settle/pallas_call | solution.py:509
  (1 shorter events, 0.0 us)

commit v6 on v5

--- a/solution.py
+++ b/solution.py
@@ -71,7 +71,7 @@
         acc = weigh(top, h, vc, v_ref, s_ref.at[rs])
         den = acc[:, 128:]
         q_ref[rs, col] = (acc[:, :128] * (1.0 / den)).astype(BF16)
-        lse_ref[rs, :] = jnp.where(lane == h, top + jnp.log2(den), lse_ref[rs, :])
+        lse_ref[rs, :] = jnp.where(lane == h % 2, top + jnp.log2(den), lse_ref[rs, :])
 
 
 def step_kernel(n_tp, pre_ref, x_hbm, wq_hbm, wk_hbm, wv_hbm, wo_hbm, gain_ref, cos_ref, sin_ref, ck_hbm, cv_hbm,
@@ -155,8 +155,58 @@
     def w_hop(k):
         hop(lambda o: wf.at[o, js, :], lambda d, i: w_s.at[d * last + i], lambda d, i: w_r.at[d * last + i], k)
 
-    def o_hop(b, k):
-        hop(lambda o: o_all.at[o, b], lambda d, i: z_s.at[b, d * last + i], lambda d, i: z_r.at[b, d * last + i], k)
+    def o_copy(u, origin, slot, to):
+        ref = o_all.at[origin, u % 2, u // 2]
+        return remote(ref, ref, z_s.at[u, slot], z_r.at[u, slot], tp=to)
+
+    sends = [(1, 0), (-1, 1), (2, 2), (-2, 3)]
+
+    def o_send(u):
+        for d, slot in sends:
+            @pl.when((z + d >= 0) & (z + d <= last))
+            def _():
+                o_copy(u, z, slot, z + d).start()
+
+    def o_pass(u):
+        @pl.when(z == 2)
+        def _():
+            o_copy(u, 0, 2, z).wait_recv()
+            o_copy(u, 0, 4, 3).start()
+
+        @pl.when(z == 1)
+        def _():
+            o_copy(u, 3, 3, z).wait_recv()
+            o_copy(u, 3, 5, 0).start()
+
+    def o_wait(u):
+        for d, slot in sends:
+            taken = (z == 2) if slot == 2 else (z == 1) if slot == 3 else (z < 0)
+
+            @pl.when((z - d >= 0) & (z - d <= last) & jnp.logical_not(taken))
+            def _():
+                o_copy(u, z - d, slot, z).wait_recv()
+
+        @pl.when(z == 3)
+        def _():
+            o_copy(u, 0, 4, z).wait_recv()
+
+        @pl.when(z == 0)
+        def _():
+            o_copy(u, 3, 5, z).wait_recv()
+
+    def o_sent(u):
+        for d, slot in sends:
+            @pl.when((z + d >= 0) & (z + d <= last))
+            def _():
+                o_copy(u, z, slot, z).wait_send()
+
+        @pl.when(z == 2)
+        def _():
+            o_copy(u, 0, 4, z).wait_send()
+
+        @pl.when(z == 1)
+        def _():
+            o_copy(u, 3, 5, z).wait_send()
 
     w_local.wait()
     w_hop(1)
@@ -230,12 +280,12 @@
         def _():
             project(g)
 
-        @pl.when(g > 0)
-        def _():
-            normalize(g - 1)
+        @pl.when(g > 1)
+        def _():
+            normalize(g - 2)
         return 0
 
-    lax.fori_loop(0, groups + 1, front, 0)
+    lax.fori_loop(0, groups + 2, front, 0)
 
     n_out = rows * toks * heads
     outs = [pltpu.make_async_copy(raw.at[0, i, pl.ds(0, n_out), :], dst, out_sem.at[groups + i]) for i, dst in enumerate((ok_hbm, ov_hbm))]
@@ -263,8 +313,9 @@
     def w_send(k, t, ref, **dev):
         return remote(ref, ref, w_s.at[nw + k + t], w_r.at[nw + k + t], **dev)
 
-    def w_y(t):
-        return w_send(0, t, wf.at[t, wslice(dp, me), :], cp=counter)
+    def w_y(i):
+        half = piece // 2
+        return w_send(3 * n_tp + 4, i, wf.at[i // 2, pl.ds(pl.multiple_of((dp * 4 + me) * piece + (i % 2) * half, half), half), :], cp=counter)
 
     def w_x_own():
         return w_send(n_tp, 0, wf.at[:, wslice(dp, me), :], dp=1 - dp)
@@ -289,52 +340,58 @@
 
     forward_q(0)
 
-    def p_copy(b, i):
+    half_w = width // 2
+
+    def pair_of(u):
+        return pl.ds(pl.multiple_of((u % 2) * half_w, half_w), half_w)
+
+    def p_copy(u, i):
         if i < 4:
             s = 1 if i < 2 else 3
-            src = (q_buf.at[b, pl.ds(s * toks, toks), :], l_buf.at[b, :, pl.ds(s * toks, toks)])[i % 2]
+            src = (q_buf.at[u // 2, pl.ds(s * toks, toks), pair_of(u)], l_buf.at[u, :, pl.ds(s * toks, toks)])[i % 2]
         else:
-            src = (c_o.at[b], c_l.at[b])[i % 2]
-        dst = (rA.at[b], lA.at[b], rB.at[b], lB.at[b], rC.at[b], lC.at[b])[i]
-        return remote(src, dst, p_s.at[b, i], p_r.at[b, i], cp=partner if i < 4 else counter)
+            src = (c_o.at[u], c_l.at[u])[i % 2]
+        dst = (rA.at[u], lA.at[u], rB.at[u], lB.at[u], rC.at[u], lC.at[u])[i]
+        return remote(src, dst, p_s.at[u, i], p_r.at[u, i], cp=partner if i < 4 else counter)
 
     def blend(parts, dst):
         top = functools.reduce(jnp.maximum, [e for _, e in parts])
         ws = [jnp.exp2(e - top) for _, e in parts]
         den = functools.reduce(jnp.add, ws)
         cols = [jnp.transpose(w / den) for w in ws]
-        for h in range(heads):
+        for h in range(half_w // 128):
             hs = slice(h * 128, (h + 1) * 128)
             acc = functools.reduce(jnp.add, [c[:, h:h + 1] * v[:, hs].astype(F32) for c, (v, _) in zip(cols, parts)])
             dst[:, hs] = acc.astype(BF16)
         return top + jnp.log2(den)
 
-    def precombine(b):
-        p_copy(b, 2).wait_recv()
-        p_copy(b, 3).wait_recv()
-        c_l[b] = blend([(q_buf.at[b, pl.ds(2 * toks, toks), :], l_buf[b, :, 2 * toks:3 * toks]), (rB.at[b], lB[b])], c_o.at[b])
-        p_copy(b, 4).start()
-        p_copy(b, 5).start()
-
-    def finish(b):
+    def precombine(u):
+        p_copy(u, 2).wait_recv()
+        p_copy(u, 3).wait_recv()
+        c_l[u] = blend([(q_buf.at[u // 2, pl.ds(2 * toks, toks), pair_of(u)], l_buf[u, :, 2 * toks:3 * toks]), (rB.at[u], lB[u])], c_o.at[u])
+        p_copy(u, 4).start()
+        p_copy(u, 5).start()
+
+    def finish(u):
         for i in (0, 1, 4, 5):
-            p_copy(b, i).wait_recv()
-        blend([(q_buf.at[b, pl.ds(0, toks), :], l_buf[b, :, 0:toks]), (rA.at[b], lA[b]), (rC.at[b], lC[b])], o_all.at[z, b])
-        o_hop(b, 1)
+            p_copy(u, i).wait_recv()
+        blend([(q_buf.at[u // 2, pl.ds(0, toks), pair_of(u)], l_buf[u, :, 0:toks]), (rA.at[u], lA[u]), (rC.at[u], lC[u])], o_all.at[z, u % 2, u // 2])
+        o_send(u)
 
     def out_copy(g):
         return pltpu.make_async_copy(x_v.at[pl.ds(2 * g, 2)], out_hbm.at[pl.ds(2 * g, 2)], out_sem.at[g])
 
     def project_out(g):
-        o_hop(2 * g, 4)
-        o_hop(2 * g + 1, 4)
+        for i in range(4):
+            o_wait(4 * g + i)
 
         def chunk(n, ss):
             cols = pl.ds(pl.multiple_of(n * 512, 512), 512)
             y = None
             for t in range(n_tp):
-                d = jnp.dot(o_all[t, pl.ds(2 * g, 2)].reshape(gt, width), wf[t, :, cols], preferred_element_type=F32)
-                y = d if y is None else y + d
+                for i in range(2):
+                    d = jnp.dot(o_all[t, i, pl.ds(2 * g, 2)].reshape(gt, half_w), wf[t, i * half_w:(i + 1) * half_w, cols], preferred_element_type=F32)
+                    y = d if y is None else y + d
             s_scr[0:gt, cols] = y
             return ss + jnp.sum(y * y, axis=1, keepdims=True)
 
@@ -374,84 +431,88 @@
                 col = pl.ds(pl.multiple_of(h * 128, 128), 128)
                 attend_head(h, q_buf.at[b], kn[b, :, col], vn[b, :, col], k_scr, v_scr, s_scr, limit, bias, lse_scr)
 
-            @pl.when(h == 0)
-            def _():
-                @pl.when((b >= 1) & (b < rows + 1))
-                def _():
-                    precombine(b - 1)
-
-                @pl.when((b >= 1) & (b < 1 + n_tp))
-                def _():
-                    w_y(b - 1).start()
-
-                @pl.when((b >= 2) & (b < 2 + n_tp))
-                def _():
-                    w_y(b - 2).wait_recv()
-                    w_x_fwd(b - 2).start()
-                    w_d_fwd(b - 2).start()
-
-                @pl.when((b >= 3) & (b < rows + 3))
-                def _():
-                    o_hop(b - 3, 3)
-
-                @pl.when(b == rows + 2)
-                def _():
-                    interleave()
-
-            @pl.when(h == 1)
-            def _():
-                @pl.when((b >= 2) & (b < rows + 2))
-                def _():
-                    o_hop(b - 2, 2)
-
-                @pl.when(b == 0)
-                def _():
-                    w_hop(3)
-
-                @pl.when(b == rows)
-                def _():
-                    w_d_own().wait_recv()
-                    for t in range(n_tp):
-                        w_d_fwd(t).wait_recv()
-                    for i in range(2):
-                        w_d_far(i).wait_recv()
-
-            @pl.when(h == 2)
-            def _():
-                @pl.when((b >= 1) & (b < rows + 1))
-                def _():
-                    finish(b - 1)
-
-            @pl.when(h == 3)
-            def _():
-                @pl.when(b == 0)
-                def _():
-                    w_hop(4)
-                    w_x_own().start()
-                    w_d_own().start()
-
-                @pl.when(b == rows - 1)
-                def _():
-                    w_x_own().wait_recv()
-                    for t in range(n_tp):
-                        w_x_fwd(t).wait_recv()
-                    for i in range(2):
-                        w_d_far(i).start()
-
-            turn = b * heads + h - (rows * heads + 1)
-
-            @pl.when((turn >= 0) & (turn % 2 == 0) & (turn < 2 * groups - 2) | (turn == 2 * groups))
-            def _():
-                project_out(jnp.minimum(turn // 2, groups - 1))
+            turn = b * heads + h
+            odd = turn % 2 == 1
+            n_u = 2 * rows
+
+            even = turn % 2 == 0
+
+            u_send = (turn - 1) // 2
+
+            @pl.when(odd & (u_send < n_u))
+            def _():
+                l_buf[u_send] = jnp.transpose(lse_scr[...])[0:8, :]
+                for i in range(4):
+                    p_copy(u_send, i).start()
+
+            u_pre = (turn - 2) // 2
+
+            @pl.when(even & (turn >= 2) & (u_pre < n_u))
+            def _():
+                precombine(u_pre)
+
+            u_fin = (turn - 5) // 2
+
+            @pl.when(odd & (turn >= 5) & (u_fin < n_u))
+            def _():
+                finish(u_fin)
+
+            u_far = (turn - 8) // 2
+
+            @pl.when(even & (turn >= 8) & (u_far < n_u))
+            def _():
+                o_pass(u_far)
+
+            @pl.when((b >= 2) & (b < 2 + n_tp) & even)
+            def _():
+                w_y((b - 2) * 2 + h // 2).start()
+
+            @pl.when((b >= 3) & (b < 3 + n_tp) & (h == 1))
+            def _():
+                t = b - 3
+                w_y(2 * t).wait_recv()
+                w_y(2 * t + 1).wait_recv()
+                w_x_fwd(t).start()
+                w_d_fwd(t).start()
+
+            @pl.when(turn == 3)
+            def _():
+                w_hop(3)
+
+            @pl.when(turn == heads + 3)
+            def _():
+                w_hop(4)
+                w_x_own().start()
+                w_d_own().start()
+
+            @pl.when(turn == rows * heads - 2)
+            def _():
+                w_x_own().wait_recv()
+                for t in range(n_tp):
+                    w_x_fwd(t).wait_recv()
+                for i in range(2):
+                    w_d_far(i).start()
+
+            @pl.when(turn == rows * heads + 1)
+            def _():
+                w_d_own().wait_recv()
+                for t in range(n_tp):
+                    w_d_fwd(t).wait_recv()
+                for i in range(2):
+                    w_d_far(i).wait_recv()
+
+            @pl.when(turn == rows * heads + 7)
+            def _():
+                interleave()
+
+            lag = turn - (rows * heads + 1)
+
+            @pl.when((lag == 0) | (lag == 3) | (lag == 4) | (lag == 7))
+            def _():
+                project_out((lag + 2) // 3)
             return 0
 
         lax.fori_loop(0, heads, head, 0)
-
-        @pl.when(b < rows)
-        def _():
-            l_buf[b] = jnp.transpose(lse_scr[...])[0:8, :]
-            for i in range(4):
-                p_copy(b, i).start()
         return 0
 
     lax.fori_loop(0, rows + 3, row, 0)
@@ -471,15 +532,16 @@
     def sent_b(b, _):
         for i in range(6):
             p_copy(b, i).wait_send()
-        hop_sent(lambda o: o_all.at[o, b], lambda d, i: z_s.at[b, d * last + i], lambda d, i: z_r.at[b, d * last + i])
+        o_sent(b)
         return 0
 
-    lax.fori_loop(0, rows, sent_b, 0)
+    lax.fori_loop(0, 2 * rows, sent_b, 0)
     hop_sent(lambda o: wf.at[o, js, :], lambda d, i: w_s.at[d * last + i], lambda d, i: w_r.at[d * last + i])
     w_x_own().wait_send()
     w_d_own().wait_send()
     for t in range(n_tp):
-        w_y(t).wait_send()
+        w_y(2 * t).wait_send()
+        w_y(2 * t + 1).wait_send()
         w_x_fwd(t).wait_send()
         w_d_fwd(t).wait_send()
     for i in range(2):
@@ -534,16 +596,16 @@
         scratch = [
             pltpu.VMEM((rows, toks, model), BF16), pltpu.VMEM((3, model, width), BF16), pltpu.VMEM((n_tp, width, model), BF16),
             pltpu.VMEM((rows, n_q, width), BF16), pltpu.VMEM((rows, toks, width), BF16), pltpu.VMEM((rows, toks, width), BF16),
-            pltpu.VMEM((rows, toks, width), BF16), pltpu.VMEM((rows, toks, width), BF16), pltpu.VMEM((rows, toks, width), BF16),
-            pltpu.VMEM((rows, 8, toks), F32), pltpu.VMEM((rows, 8, toks), F32), pltpu.VMEM((rows, 8, toks), F32),
-            pltpu.VMEM((rows, toks, width), BF16), pltpu.VMEM((rows, 8, toks), F32), pltpu.VMEM((rows, 8, n_q), F32),
-            pltpu.VMEM((n_tp, rows, toks, width), BF16), pltpu.VMEM((rows // 2, n_tp, 8, 2 * toks), F32),
+            pltpu.VMEM((2 * rows, toks, width // 2), BF16), pltpu.VMEM((2 * rows, toks, width // 2), BF16), pltpu.VMEM((2 * rows, toks, width // 2), BF16),
+            pltpu.VMEM((2 * rows, 8, toks), F32), pltpu.VMEM((2 * rows, 8, toks), F32), pltpu.VMEM((2 * rows, 8, toks), F32),
+            pltpu.VMEM((2 * rows, toks, width // 2), BF16), pltpu.VMEM((2 * rows, 8, toks), F32), pltpu.VMEM((2 * rows, 8, n_q), F32),
+            pltpu.VMEM((n_tp, 2, rows, toks, width // 2), BF16), pltpu.VMEM((rows // 2, n_tp, 8, 2 * toks), F32),
             pltpu.VMEM((2, 2, slots * heads, dim), BF16), pltpu.VMEM((1024, 128), F32),
             pltpu.VMEM((heads, slots, dim), BF16), pltpu.VMEM((heads, slots, 2 * dim), BF16),
             pltpu.VMEM((n_q, slots + toks), F32), pltpu.VMEM((n_q, toks), F32), pltpu.VMEM((n_q, 128), F32),
             dma((4 + rows // 2,)), dma((2, 2)), dma((rows // 2 + 2,)), dma((rows // 2, last)), dma((rows // 2, last)),
-            dma((rows, 3)), dma((rows, 3)), dma((rows, 6)), dma((rows, 6)), dma((rows, 2 * last)), dma((rows, 2 * last)),
-            dma((2 * last + 3 * n_tp + 4,)), dma((2 * last + 3 * n_tp + 4,)),
+            dma((rows, 3)), dma((rows, 3)), dma((2 * rows, 6)), dma((2 * rows, 6)), dma((2 * rows, 2 * last)), dma((2 * rows, 2 * last)),
+            dma((2 * last + 5 * n_tp + 4,)), dma((2 * last + 5 * n_tp + 4,)),
         ]
         flops = 2 * rows * toks * model * width * 3 + 4 * rows * n_q * slots * width + 2 * rows * toks * model * model
         out, ok, ov = pl.pallas_call(

time: 151 us -> 147 us (0.974)
  Pallas kernels: 144 us -> 140 us
    pallas_call x1, Pallas kernels: 138 us -> 134 us  [local_step(): pl.pallas_call(functools.partial(step_kernel, n_tp), in_specs=[pl.BlockSp...]
where the time goes in v6:
time: 147 us
  Pallas kernels  140 us (95%)
  other arithmetic  4.56 us (3%)
  local copies, waits for them, and re-layouts  2.06 us (1%)
    pallas_call x1, Pallas kernels, local_step(): pl.pallas_call(functools.partial(step_kernel, n_tp), in_specs=[pl.BlockSp...  134 us
    pallas_call x1, Pallas kernels, settle(): pl.pallas_call(functools.partial(settle_kernel, n), in_specs=[any_] * n,...  5.64 us

profile of v6, /device:TPU:0, one launch (start us, length us, event | category | flops | bytes accessed | tf_op | source)
XLA Modules:
  0.0 147.1 jit_solution(10963186283987504229)
XLA Ops:
  0.6 0.7 broadcast_add_fusion
  1.3 0.7 concatenate.22
  2.0 0.7 concatenate.23
  2.7 0.1 add_convert_fusion
  2.7 0.7 concatenate.24
  3.4 0.6 maximum_convert_fusion.gain_ref
  4.1 1.9 %fusion = (f32[8,128,64]{2,1,0:T(8,128)S(1)}, f32[8,128,64]{2,1,0:T(8,128)S(1)}, f32[8,128,64]{2,1,0:T(8,128)S(1)}) fusion(f32[64]{0:T(128)S(1)} %negate_power_fusion, f32[8,128]{1,0:T(8,128)S(1)} %add_convert_fusion), kind=kLoop, calls=%fused_computation.4 | loop fusion | flops 131072 | bytes 790784 | tf_op jit(solution)/shard_map/neg | solution.py:591
  6.0 1.3 pad_maximum_fusion
  7.3 134.2 %step.1 = (bf16[8,128,2048]{2,1,0:T(8,128)(2,1)}, bf16[4096,128]{1,0:T(8,128)(2,1)}, bf16[4096,128]{1,0:T(8,128)(2,1)}) custom-call(s32[8]{0:T(128)} %pre_ref.1, bf16[8,128,2048]{2,1,0:T(8,128)(2,1)} %x_hbm.1, bf16[2048,512]{1,0:T(8,128)(2,1)} %wq_hbm.1, bf16[2048,512]{1,0:T(8,128)(2,1)} %wk_hbm.1, bf16[2048,512]{1,0:T(8,128)(2,1)} %wv_hbm.1, ...), custom_call_target="tpu_custom_call" | custom-call | flops 32212254720 | bytes 33554432 | tf_op jit(solution)/shard_map/step/pallas_call | solution.py:611
  141.5 5.6 %settle.1 = (bf16[8,128,2048]{2,1,0:T(8,128)(2,1)}, bf16[4096,128]{1,0:T(8,128)(2,1)}, bf16[4096,128]{1,0:T(8,128)(2,1)}) custom-call(bf16[8,128,2048]{2,1,0:T(8,128)(2,1)} %get-tuple-element.9.refs_0_, bf16[4096,128]{1,0:T(8,128)(2,1)} %get-tuple-element.10.refs_1_, bf16[4096,128]{1,0:T(8,128)(2,1)} %get-tuple-element.11.refs_2_), custom_call_target="tpu_custom_call" | custom-call | tf_op jit(solution)/shard_map/settle/pallas_call | solution.py:571
  (1 shorter events, 0.0 us)

commit v7 on v6

--- a/solution.py
+++ b/solution.py
@@ -16,24 +16,29 @@
 BF16 = jnp.bfloat16
 
 
-def split_heads(raw_ref, wide_ref, out_ref, heads, rows):
-    step = wide_ref.shape[0]
+def split_quarter(part, raw_ref, wide_ref, outs):
+    heads, slots = outs[0].shape[0], outs[0].shape[1]
+    step = wide_ref.shape[1]
     per = step // heads
-
-    def body(i, _):
-        wide_ref[...] = raw_ref[pl.ds(i * step, step), :].astype(F32)
-        for h in range(heads):
-            out_ref[h, pl.ds(i * per, per), 0:128] = wide_ref[pl.ds(h, per, stride=heads), :].astype(BF16)
-        return 0
-
-    lax.fori_loop(0, rows // step, body, 0)
+    quarter = slots // 4
+    for t, out_ref in enumerate(outs):
+        for i in range(quarter // per):
+            w = wide_ref.at[t * (quarter // per) + i]
+            at = part * quarter + i * per
+            for n in range(4):
+                rs = pl.ds(pl.multiple_of(at * heads + n * (step // 4), step // 4), step // 4)
+                w[n * (step // 4):(n + 1) * (step // 4), :] = raw_ref[t, rs, :].astype(F32)
+                yield
+            for h in range(heads):
+                out_ref[h, pl.ds(pl.multiple_of(at, per), per), :] = w[pl.ds(h, per, stride=heads), :].astype(BF16)
+                yield
 
 
 SCALE = (128 ** -0.5) * LOG2E
 TILE = 256
 
 
-def scores(q, h, kc, bias, k_ref, s_ref, limit):
+def scores(q, h, kc, bias, k_ref, s_ref, limit, side):
     n_t = k_ref.shape[1] // TILE
     lane = lax.broadcasted_iota(jnp.int32, (1, TILE), 1)
     s = lax.dot_general(q, kc, NT, preferred_element_type=F32)
@@ -46,41 +51,44 @@
         s_ref[:, j * TILE:(j + 1) * TILE] = s
         for u in range(TILE // 128):
             mx = jnp.maximum(mx, s[:, u * 128:(u + 1) * 128])
+        next(side, None)
     return jnp.max(mx, axis=1, keepdims=True) * SCALE
 
 
-def weigh(top, h, vc, v_ref, s_ref):
+def weigh(top, h, vc, v_ref, s_ref, side):
     n_t = v_ref.shape[1] // TILE
     acc = None
     for j in range(n_t):
         p = jnp.exp2(s_ref[:, j * TILE:(j + 1) * TILE] * SCALE - top)
-        d = jnp.dot(p.astype(BF16), v_ref[h, j * TILE:(j + 1) * TILE, :], preferred_element_type=F32)
+        v = v_ref[h, j * TILE:(j + 1) * TILE, :]
+        d = jnp.dot(p.astype(BF16), jnp.concatenate([v, jnp.ones(v.shape, BF16)], axis=1), preferred_element_type=F32)
         acc = d if acc is None else acc + d
+        next(side, None)
     p = jnp.exp2(s_ref[:, n_t * TILE:n_t * TILE + 128] * SCALE - top)
     return acc + jnp.dot(p.astype(BF16), vc, preferred_element_type=F32)
 
 
-def attend_head(h, q_ref, kc, vc, k_ref, v_ref, s_ref, limit, bias_ref, lse_ref):
+def attend_head(h, q_ref, kc, vc, k_ref, v_ref, s_ref, limit, bias_ref, lse_ref, side):
     col = pl.ds(pl.multiple_of(h * 128, 128), 128)
     half = q_ref.shape[0] // 2
     vc = jnp.concatenate([vc, jnp.ones(vc.shape, BF16)], axis=1)
     parts = [slice(r * half, (r + 1) * half) for r in range(2)]
-    tops = [scores(q_ref[rs, col], h, kc, bias_ref[rs, :], k_ref, s_ref.at[rs], limit) for rs in parts]
+    tops = [scores(q_ref[rs, col], h, kc, bias_ref[rs, :], k_ref, s_ref.at[rs], limit, side) for rs in parts]
     lane = lax.broadcasted_iota(jnp.int32, (half, 128), 1)
     for rs, top in zip(parts, tops):
-        acc = weigh(top, h, vc, v_ref, s_ref.at[rs])
+        acc = weigh(top, h, vc, v_ref, s_ref.at[rs], side)
         den = acc[:, 128:]
         q_ref[rs, col] = (acc[:, :128] * (1.0 / den)).astype(BF16)
         lse_ref[rs, :] = jnp.where(lane == h % 2, top + jnp.log2(den), lse_ref[rs, :])
 
 
-def step_kernel(n_tp, pre_ref, x_hbm, wq_hbm, wk_hbm, wv_hbm, wo_hbm, gain_ref, cos_ref, sin_ref, ck_hbm, cv_hbm,
+def step_kernel(n_tp, pre_ref, x_hbm, wq_hbm, wk_hbm, wv_hbm, wo_hbm, qg_ref, kg_ref, pg_ref, freq_ref, ck_hbm, cv_hbm,
                 out_hbm, ok_hbm, ov_hbm,
                 x_v, wqkv, wf, q_buf, kn, vn, rA, rB, rC, lA, lB, lC, c_o, c_l, l_buf, o_all, st,
-                raw, wide, k_scr, v_scr, s_scr, bias, lse_scr,
+                raw, cos_ref, sin_ref, wide, k_even, v_even, k_odd, v_odd, s_scr, bias, lse_scr,
                 in_sem, kv_sem, out_sem, st_s, st_r, q_s, q_r, p_s, p_r, z_s, z_r, w_s, w_r):
     rows, toks, model = x_v.shape
-    heads, slots = k_scr.shape[0], k_scr.shape[1]
+    heads, slots = k_even.shape[0], k_even.shape[1]
     width = heads * 128
     groups = rows // 2
     gt = 2 * toks
@@ -113,8 +121,9 @@
         return (pltpu.make_async_copy(ck_hbm.at[b], raw.at[par, 0], kv_sem.at[par, 0]),
                 pltpu.make_async_copy(cv_hbm.at[b], raw.at[par, 1], kv_sem.at[par, 1]))
 
-    for cpy in kv_copies(0):
-        cpy.start()
+    for r in range(2):
+        for cpy in kv_copies(r):
+            cpy.start()
 
     barrier = pltpu.get_barrier_semaphore()
     for i in range(1, n_tp):
@@ -216,7 +225,21 @@
     for s, blk in enumerate((me, partner, counter, diag)):
         bias[s * toks:(s + 1) * toks, :] = jnp.where(ki - qi <= (blk - me) * toks, 0.0, -1.0)
     lse_scr[...] = jnp.zeros(lse_scr.shape, F32)
-    v_scr[:, :, 128:] = jnp.ones((heads, slots, 128), BF16)
+
+    low = lax.broadcasted_iota(jnp.int32, (toks, 128), 1) < 64
+
+    def tables(i, _):
+        start = jnp.where(low, pre_ref[2 * i], pre_ref[2 * i + 1]) + me * toks
+        angle = (start + lax.broadcasted_iota(jnp.int32, (toks, 128), 0)).astype(F32) * freq_ref[0:1, :]
+        c, s = jnp.cos(angle), jnp.sin(angle)
+        c_far, s_far = pltpu.roll(c, 64, 1), pltpu.roll(s, 64, 1)
+        cos_ref[2 * i] = jnp.where(low, c, c_far)
+        cos_ref[2 * i + 1] = jnp.where(low, c_far, c)
+        sin_ref[2 * i] = jnp.where(low, -s, s_far)
+        sin_ref[2 * i + 1] = jnp.where(low, -s_far, s)
+        return 0
+
+    lax.fori_loop(0, groups, tables, 0)
 
     def st_copy(g, i):
         return remote(st.at[g, 0], st.at[g, i], st_s.at[g, i - 1], st_r.at[g, i - 1], tp=(z + i) % n_tp)
@@ -260,10 +283,10 @@
         for i in range(1, n_tp):
             tot = tot + st[g, i]
         inv = jnp.transpose(lax.rsqrt(tot / (width * n_tp) + NORM_EPS))
-        for t, (gain, base) in enumerate(((0, 0), (width, gt))):
+        for t, (gain, base) in enumerate(((qg_ref, 0), (kg_ref, gt))):
             for h in range(heads):
                 u = s_scr[base:base + gt, pl.ds(pl.multiple_of(g * width + h * 128, 128), 128)]
-                u = u * inv[:, t:t + 1] * gain_ref[0:1, gain + h * 128:gain + (h + 1) * 128]
+                u = u * inv[:, t:t + 1] * gain[0:1, h * 128:(h + 1) * 128]
                 cos = cos_ref[pl.ds(2 * g, 2)].reshape(gt, 128)
                 sin = sin_ref[pl.ds(2 * g, 2)].reshape(gt, 128)
                 u = (u * cos + pltpu.roll(u, 64, 1) * sin).astype(BF16).reshape(2, toks, 128)
@@ -296,9 +319,9 @@
         def one(r, _):
             for i, src in enumerate((kn, vn)):
                 for h in range(heads):
-                    wide[pl.ds(i * per + h, toks, stride=heads), :] = src[r, :, h * 128:(h + 1) * 128].astype(F32)
+                    wide[0, pl.ds(i * per + h, toks, stride=heads), :] = src[r, :, h * 128:(h + 1) * 128].astype(F32)
             for i in range(2):
-                raw[0, i, pl.ds(pl.multiple_of(r * per, per), per), :] = wide[i * per:(i + 1) * per, :].astype(BF16)
+                raw[0, i, pl.ds(pl.multiple_of(r * per, per), per), :] = wide[0, i * per:(i + 1) * per, :].astype(BF16)
             return 0
 
         lax.fori_loop(0, rows, one, 0)
@@ -399,25 +422,35 @@
         inv = lax.rsqrt(ss / model + NORM_EPS)
         for n in range(model // 512):
             cols = slice(n * 512, (n + 1) * 512)
-            y = s_scr[0:gt, cols] * inv * gain_ref[0:1, 2 * width + n * 512:2 * width + (n + 1) * 512]
+            y = s_scr[0:gt, cols] * inv * pg_ref[0:1, n * 512:(n + 1) * 512]
             y = x_v[pl.ds(2 * g, 2), :, cols].reshape(gt, 512).astype(F32) + y
             x_v[pl.ds(2 * g, 2), :, cols] = y.astype(BF16).reshape(2, toks, 512)
         out_copy(g).start()
 
+    for cpy in kv_copies(0):
+        cpy.wait()
+
+    def first_row(h, _):
+        for _ in split_quarter(h, raw.at[0], wide, (k_even, v_even)):
+            pass
+        return 0
+
+    lax.fori_loop(0, heads, first_row, 0)
+
     def row(b, _):
         @pl.when(b < rows)
         def _():
-            for cpy in kv_copies(b):
-                cpy.wait()
-
             @pl.when(b + 1 < rows)
             def _():
                 for cpy in kv_copies(b + 1):
+                    cpy.wait()
+                forward_q(b + 1)
+
+            @pl.when(b + 2 < rows)
+            def _():
+                for cpy in kv_copies(b + 2):
                     cpy.start()
-                forward_q(b + 1)
-
-            split_heads(raw.at[b % 2, 0], wide, k_scr, heads, slots * heads)
-            split_heads(raw.at[b % 2, 1], wide, v_scr, heads, slots * heads)
+
             for i in (0, 2):
                 q_copy(b, i).wait_recv()
             for i in range(3):
@@ -426,10 +459,14 @@
         limit = pre_ref[jnp.minimum(b, rows - 1)] - me * slots
 
         def head(h, _):
-            @pl.when(b < rows)
-            def _():
-                col = pl.ds(pl.multiple_of(h * 128, 128), 128)
-                attend_head(h, q_buf.at[b], kn[b, :, col], vn[b, :, col], k_scr, v_scr, s_scr, limit, bias, lse_scr)
+            col = pl.ds(pl.multiple_of(h * 128, 128), 128)
+            for parity, now, nxt in ((0, (k_even, v_even), (k_odd, v_odd)), (1, (k_odd, v_odd), (k_even, v_even))):
+                @pl.when((b < rows) & (b % 2 == parity))
+                def _():
+                    side = split_quarter(h, raw.at[1 - parity], wide, nxt)
+                    attend_head(h, q_buf.at[b], kn[b, :, col], vn[b, :, col], now[0], now[1], s_scr, limit, bias, lse_scr, side)
+                    for _ in side:
+                        pass
 
             turn = b * heads + h
             odd = turn % 2 == 1
@@ -583,12 +620,8 @@
         slots, heads, dim = cache_k.shape[1:]
         width = heads * dim
         n_q = 4 * toks
-        positions = prefix_len[:, None] + lax.axis_index('cp') * toks + jnp.arange(toks, dtype=jnp.int32)[None, :]
         inv_freq = ROPE_BASE ** (-(jnp.arange(dim // 2, dtype=F32) * 2.0 / dim))
-        angles = positions.astype(F32)[..., None] * inv_freq
-        cos, sin = jnp.cos(angles), jnp.sin(angles)
-        cos = jnp.concatenate([cos, cos], axis=-1)
-        sin = jnp.concatenate([-sin, sin], axis=-1)
+        freq = jnp.concatenate([inv_freq, inv_freq]).reshape(1, dim)
         any_ = pl.BlockSpec(memory_space=pl.ANY)
         vm = pl.BlockSpec(memory_space=pltpu.VMEM)
         dma = pltpu.SemaphoreType.DMA
@@ -600,8 +633,8 @@
             pltpu.VMEM((2 * rows, 8, toks), F32), pltpu.VMEM((2 * rows, 8, toks), F32), pltpu.VMEM((2 * rows, 8, toks), F32),
             pltpu.VMEM((2 * rows, toks, width // 2), BF16), pltpu.VMEM((2 * rows, 8, toks), F32), pltpu.VMEM((2 * rows, 8, n_q), F32),
             pltpu.VMEM((n_tp, 2, rows, toks, width // 2), BF16), pltpu.VMEM((rows // 2, n_tp, 8, 2 * toks), F32),
-            pltpu.VMEM((2, 2, slots * heads, dim), BF16), pltpu.VMEM((1024, 128), F32),
-            pltpu.VMEM((heads, slots, dim), BF16), pltpu.VMEM((heads, slots, 2 * dim), BF16),
+            pltpu.VMEM((2, 2, slots * heads, dim), BF16), pltpu.VMEM((rows, toks, dim), F32), pltpu.VMEM((rows, toks, dim), F32), pltpu.VMEM((4, 1024, 128), F32),
+            pltpu.VMEM((heads, slots, dim), BF16), pltpu.VMEM((heads, slots, dim), BF16), pltpu.VMEM((heads, slots, dim), BF16), pltpu.VMEM((heads, slots, dim), BF16),
             pltpu.VMEM((n_q, slots + toks), F32), pltpu.VMEM((n_q, toks), F32), pltpu.VMEM((n_q, 128), F32),
             dma((4 + rows // 2,)), dma((2, 2)), dma((rows // 2 + 2,)), dma((rows // 2, last)), dma((rows // 2, last)),
             dma((rows, 3)), dma((rows, 3)), dma((2 * rows, 6)), dma((2 * rows, 6)), dma((2 * rows, 2 * last)), dma((2 * rows, 2 * last)),
@@ -610,15 +643,15 @@
         flops = 2 * rows * toks * model * width * 3 + 4 * rows * n_q * slots * width + 2 * rows * toks * model * model
         out, ok, ov = pl.pallas_call(
             functools.partial(step_kernel, n_tp),
-            in_specs=[pl.BlockSpec(memory_space=pltpu.SMEM)] + [any_] * 5 + [vm] * 3 + [any_] * 2,
+            in_specs=[pl.BlockSpec(memory_space=pltpu.SMEM)] + [any_] * 5 + [vm] * 4 + [any_] * 2,
             out_specs=[any_] * 3,
             out_shape=[jax.ShapeDtypeStruct((rows, toks, model), BF16), jax.ShapeDtypeStruct((rows * toks * heads, dim), BF16), jax.ShapeDtypeStruct((rows * toks * heads, dim), BF16)],
             scratch_shapes=scratch,
             compiler_params=pltpu.CompilerParams(collective_id=0, has_side_effects=True, vmem_limit_bytes=67043328),
             cost_estimate=pl.CostEstimate(flops=flops, bytes_accessed=4 * rows * slots * width, transcendentals=rows * n_q * slots * heads),
             name="step",
-        )(prefix_len, x_chunk, w_query, w_key, w_value, w_out, jnp.concatenate([q_gain, k_gain, post_gain]).astype(F32).reshape(1, 2 * width + model),
-          cos, sin, cache_k.reshape(rows, slots * heads, dim), cache_v.reshape(rows, slots * heads, dim))
+        )(prefix_len, x_chunk, w_query, w_key, w_value, w_out, q_gain.astype(F32).reshape(1, width), k_gain.astype(F32).reshape(1, width), post_gain.astype(F32).reshape(1, model), freq,
+          cache_k.reshape(rows, slots * heads, dim), cache_v.reshape(rows, slots * heads, dim))
         out, ok, ov = settle((out, ok, ov))
         return out, ok.reshape(rows, toks, heads, dim), ov.reshape(rows, toks, heads, dim)
 

time: 147 us -> 141 us (0.959)
  Pallas kernels: 140 us -> 136 us
  local copies, waits for them, and re-layouts: 2.06 us -> 0 us
    reshape x0 -> x4, other arithmetic: none -> 4.45 us  [the longest x1 1.29 us: local_step(): post_gain.astype(F32).reshape(1, model)]
    pallas_call x1, Pallas kernels: 134 us -> 130 us  [local_step(): pl.pallas_call(functools.partial(step_kernel, n_tp), in_specs=[pl.BlockSp...]
    concatenate x3 -> x0, local copies, waits for them, and re-layouts: 2.06 us -> none  [local_step(): jnp.concatenate([q_gain, k_gain, post_gain]).astype(F32)]
    neg x1 -> x0, other arithmetic: 1.9 us -> none  [local_step(): sin = jnp.concatenate([-sin, sin], axis=-1)]
where the time goes in v7:
time: 141 us
  Pallas kernels  136 us (96%)
  other arithmetic  4.46 us (3%)
    pallas_call x1, Pallas kernels, local_step(): pl.pallas_call(functools.partial(step_kernel, n_tp), in_specs=[pl.BlockSp...  130 us
    pallas_call x1, Pallas kernels, settle(): pl.pallas_call(functools.partial(settle_kernel, n), in_specs=[any_] * n,...  5.64 us

profile of v7, /device:TPU:0, one launch (start us, length us, event | category | flops | bytes accessed | tf_op | source)
XLA Modules:
  0.0 140.6 jit_solution(11854497751269955001)
XLA Ops:
  0.6 0.7 maximum_bitcast_fusion.freq_ref
  1.3 1.3 reshape.47
  2.6 1.3 reshape.49
  3.8 1.3 reshape.51
  5.1 129.9 %step.1 = (bf16[8,128,2048]{2,1,0:T(8,128)(2,1)}, bf16[4096,128]{1,0:T(8,128)(2,1)}, bf16[4096,128]{1,0:T(8,128)(2,1)}) custom-call(s32[8]{0:T(128)} %pre_ref.1, bf16[8,128,2048]{2,1,0:T(8,128)(2,1)} %x_hbm.1, bf16[2048,512]{1,0:T(8,128)(2,1)} %wq_hbm.1, bf16[2048,512]{1,0:T(8,128)(2,1)} %wk_hbm.1, bf16[2048,512]{1,0:T(8,128)(2,1)} %wv_hbm.1, ...), custom_call_target="tpu_custom_call" | custom-call | flops 32212254720 | bytes 33554432 | tf_op jit(solution)/shard_map/step/pallas_call | solution.py:644
  135.0 5.6 %settle.1 = (bf16[8,128,2048]{2,1,0:T(8,128)(2,1)}, bf16[4096,128]{1,0:T(8,128)(2,1)}, bf16[4096,128]{1,0:T(8,128)(2,1)}) custom-call(bf16[8,128,2048]{2,1,0:T(8,128)(2,1)} %get-tuple-element.9.refs_0_, bf16[4096,128]{1,0:T(8,128)(2,1)} %get-tuple-element.10.refs_1_, bf16[4096,128]{1,0:T(8,128)(2,1)} %get-tuple-element.11.refs_2_), custom_call_target="tpu_custom_call" | custom-call | tf_op jit(solution)/shard_map/settle/pallas_call | solution.py:608
  (1 shorter events, 0.0 us)
